TPU v7x, 8 devices: a whole 2x2x1 slice. The times are simulated.
8 devices in a mesh: dp: 2 (over z, y), tp: 4 (over x, core).
Axes of the slice: x: 2, y: 2, z: 1, core: 2. Of those that a mesh axis runs over, the one named last changes fastest.
Arguments:
- hidden: bfloat16 [24, 1152, 2048], P('dp', 'tp'), parts along dimension 0
- prefix_len: int32 [24], P('dp'), parts along dimension 0
- valid_len: int32 [24], P('dp'), parts along dimension 0
- norm_attn: bfloat16 [2048], replicated
- w_query: bfloat16 [2048, 2048], P(None, 'tp')
- w_key: bfloat16 [2048, 256], replicated
- w_value: bfloat16 [2048, 256], replicated
- w_out: bfloat16 [2048, 2048], P('tp')
- norm_mlp: bfloat16 [2048], replicated
- w_gate: bfloat16 [2048, 16384], P(None, 'tp')
- w_up: bfloat16 [2048, 16384], P(None, 'tp')
- w_down: bfloat16 [16384, 2048], P('tp')
Outputs:
- output 1: bfloat16 [24, 1152, 2048], P('dp', 'tp'), parts along dimension 0
- output 2: bfloat16 [24, 1152, 256], P('dp', 'tp'), parts along dimension 0
- output 3: bfloat16 [24, 1152, 256], P('dp', 'tp'), parts along dimension 0
There are 2 independent parts. A program takes and returns all parts, laid end to end along the dimension named above; an argument that names none is the same for every part.
All inputs are finite; a program needn't handle non-finite values.
Results may differ from a plain program's by a relative error of at most 0.0131743.
Values are sent between devices in bfloat16 or wider.
A program may use at most 1 GiB of HBM per device.

v0:
```python
import jax
import jax.numpy as jnp
from jax import lax
from jax.sharding import PartitionSpec as P, NamedSharding

NORM_EPS = 1e-6
ROPE_BASE = 10000.0
MASK_FILL = -1e30


def rms_norm(acts, norm_scale):
    acts_f32 = acts.astype(jnp.float32)
    inv_rms = lax.rsqrt(jnp.mean(acts_f32 * acts_f32, axis=-1, keepdims=True) + NORM_EPS)
    return (acts_f32 * inv_rms * (1.0 + norm_scale.astype(jnp.float32))).astype(jnp.bfloat16)


def rope_tables(positions, head_dim):
    half_dim = head_dim // 2
    inv_freq = ROPE_BASE ** (-2.0 * jnp.arange(half_dim, dtype=jnp.float32) / head_dim)
    angles = positions.astype(jnp.float32)[:, None] * inv_freq[None, :]
    return jnp.cos(angles), jnp.sin(angles)


def apply_rope(vectors, cos_table, sin_table):
    half_dim = vectors.shape[-1] // 2
    first_half = vectors[..., :half_dim]
    second_half = vectors[..., half_dim:]
    return jnp.concatenate([first_half * cos_table - second_half * sin_table, second_half * cos_table + first_half * sin_table], axis=-1)


def solution(mesh):
    tp_size = mesh.shape["tp"]
    row_spec = P("dp", "tp", None)
    arg_specs = (row_spec, P("dp"), P("dp"), P(), P(None, "tp"), P(), P(), P("tp", None), P(), P(None, "tp"), P(None, "tp"), P("tp", None))

    def local_layer(hidden, prefix_len, valid_len, norm_attn, w_query, w_key, w_value, w_out, norm_mlp, w_gate, w_up, w_down):
        num_batch, local_len, d_model = hidden.shape
        head_dim = w_key.shape[1]
        local_heads = w_query.shape[1] // head_dim
        seq_len = local_len * tp_size
        row_start = lax.axis_index("tp") * local_len
        positions = jnp.arange(seq_len)
        cos_full, sin_full = rope_tables(positions, head_dim)
        cos_local = lax.dynamic_slice_in_dim(cos_full, row_start, local_len, axis=0)
        sin_local = lax.dynamic_slice_in_dim(sin_full, row_start, local_len, axis=0)
        normed = rms_norm(hidden, norm_attn)
        key_local = apply_rope(jnp.einsum("bsd,de->bse", normed, w_key, preferred_element_type=jnp.float32), cos_local, sin_local).astype(jnp.bfloat16)
        value_local = jnp.einsum("bsd,de->bse", normed, w_value, preferred_element_type=jnp.float32).astype(jnp.bfloat16)
        normed_full = lax.all_gather(normed, "tp", axis=1, tiled=True)
        key_full = lax.all_gather(key_local, "tp", axis=1, tiled=True)
        value_full = lax.all_gather(value_local, "tp", axis=1, tiled=True)
        query_rows = jnp.einsum("bsd,dn->bsn", normed_full, w_query, preferred_element_type=jnp.float32).reshape(num_batch, seq_len, local_heads, head_dim)
        query_rows = (apply_rope(query_rows, cos_full[:, None, :], sin_full[:, None, :]) * head_dim ** -0.5).astype(jnp.bfloat16)
        scores = jnp.einsum("bqhe,bke->bhqk", query_rows, key_full, preferred_element_type=jnp.float32)
        row_pos = positions[None, :, None]
        col_pos = positions[None, None, :]
        allowed = (col_pos < valid_len[:, None, None]) & ((col_pos < prefix_len[:, None, None]) | (col_pos <= row_pos))
        attn_probs = jax.nn.softmax(jnp.where(allowed[:, None], scores, MASK_FILL), axis=-1).astype(jnp.bfloat16)
        attn_vals = jnp.einsum("bhqk,bke->bqhe", attn_probs, value_full, preferred_element_type=jnp.float32).astype(jnp.bfloat16)
        attn_part = jnp.einsum("crif,ife->cre", attn_vals, w_out.reshape(local_heads, head_dim, d_model), preferred_element_type=jnp.float32).astype(jnp.bfloat16)
        attn_out = lax.psum_scatter(attn_part, "tp", scatter_dimension=1, tiled=True)
        hidden_mid = (hidden.astype(jnp.float32) + attn_out.astype(jnp.float32)).astype(jnp.bfloat16)
        normed_mlp = rms_norm(hidden_mid, norm_mlp)
        normed_mlp_full = lax.all_gather(normed_mlp, "tp", axis=1, tiled=True)
        gate_proj = jnp.einsum("bsd,df->bsf", normed_mlp_full, w_gate, preferred_element_type=jnp.float32)
        up_proj = jnp.einsum("bsd,df->bsf", normed_mlp_full, w_up, preferred_element_type=jnp.float32)
        mlp_act = (jax.nn.gelu(gate_proj, approximate=True) * up_proj).astype(jnp.bfloat16)
        mlp_part = jnp.einsum("bsf,fd->bsd", mlp_act, w_down, preferred_element_type=jnp.float32).astype(jnp.bfloat16)
        mlp_out = lax.psum_scatter(mlp_part, "tp", scatter_dimension=1, tiled=True)
        hidden_out = (hidden_mid.astype(jnp.float32) + mlp_out.astype(jnp.float32)).astype(jnp.bfloat16)
        return hidden_out, key_local, value_local

    return jax.shard_map(local_layer, mesh=mesh, in_specs=arg_specs, out_specs=(row_spec, row_spec, row_spec), check_vma=False)
```

profile of v0, /device:TPU:1, one launch (start us, length us, event | category | flops | bytes accessed | tf_op | source)
XLA Modules:
  0.0 2516.5 jit_solution(14856715293631704465)
XLA Ops:
  7.2 0.0 copy-start
  7.2 0.0 all-gather.9.cloned.1.call-start
  7.2 0.8 convert_add_fusion.3
  8.1 7.9 fusion.12
  15.9 13.5 fusion.14
  29.5 0.0 all-gather.9.cloned.1.call-update
  29.5 0.0 all-gather.7.cloned.1.call-start
  29.6 2.1 multiply_cosine_fusion
  31.7 7.5 fusion.36
  39.3 0.5 subtract_convert_fusion
  39.7 0.0 copy-start.4
  39.8 0.0 copy-start.5
  39.8 1.4 pad_maximum_fusion
  41.2 0.0 all-gather.7.cloned.1.call-update
  41.2 0.3 all-gather.5.cloned.1.call-start
  41.5 10.3 convolution_convert_fusion.1
  51.8 0.0 all-gather.5.cloned.1.call-update
  51.8 0.0 reduce-scatter.3.cloned.1.call-start
  51.9 0.4 iota_compare_fusion
  52.3 0.1 iota_compare_fusion.1
  52.4 11.8 or_and_fusion
  64.2 297.8 %all-gather.9.cloned.1.call-done = bf16[12,1152,2048]{2,1,0:T(8,128)(2,1)} async-done(((bf16[12,288,2048]{2,1,0:T(8,128)(2,1)}), bf16[12,1152,2048]{2,1,0:T(8,128)(2,1)}) %all-gather.9.cloned.1.call-update) | async-done | bytes 56623120 | tf_op jit(solution)/shard_map/all_gather | solution.py:49
  362.0 37.9 %fusion.34 = f32[12,1152,512]{1,2,0:T(8,128)} fusion(bf16[12,1152,2048]{2,1,0:T(8,128)(2,1)} %all-gather.9.cloned.1.call-done, bf16[2048,512]{1,0:T(8,128)(2,1)} %param.16), kind=kOutput, calls=%fused_computation.47 | convolution fusion | flops 28991029248 | bytes 87031808 | tf_op jit(solution)/shard_map/bsd,dn->bsn/dot_general | solution.py:52
  399.9 18.7 fusion.49
  418.6 15.1 copy.24
  433.7 15.1 copy.23
  448.8 18.5 multiply_subtract_fusion
  467.3 64.3 %fusion.50 = (f32[12,2,1152]{2,1,0:T(2,128)S(1)}, f32[12,2,1152,1152]{2,3,1,0:T(8,128)}) fusion(pred[12,1152,1152]{1,2,0:T(8,128)(4,1)} %or_and_fusion, bf16[12,1152,256]{2,1,0:T(8,128)(2,1)} %all-gather.7.cloned.1.call-done, f32[12,1152,2,128]{3,1,2,0:T(8,128)} %get-tuple-element.4, f32[12,1152,2,128]{3,1,2,0:T(8,128)} %get-tuple-element.3), kind=kOutput, calls=%fused_computation.74 | convolution fusion | flops 16424240128 | bytes 178827264 | tf_op jit(solution)/shard_map/sub | solution.py:58
  531.6 0.0 all-gather.5.cloned.1.call-done
  531.6 0.0 copy-done
  531.6 86.0 %bitcast_convert_fusion = bf16[12,1152,2048]{2,1,0:T(8,128)(2,1)} fusion(bf16[2,256,2048,1]{2,1,0,3:T(8,128)(2,1)S(1)} %bitcast.69, f32[12,2,1152,1152]{2,3,1,0:T(8,128)} %get-tuple-element.12, f32[12,2,1152]{2,1,0:T(2,128)S(1)} %get-tuple-element.11, bf16[12,1152,256]{2,1,0:T(8,128)(2,1)} %all-gather.5.cloned.1.call-done), kind=kOutput, calls=%fused_computation.15 | convolution fusion | flops 45397573632 | bytes 193310720 | tf_op jit(solution)/shard_map/crif,ife->cre/dot_general | solution.py:60
  617.7 0.0 reduce-scatter.3.cloned.1.call-update
  617.7 0.0 all-gather.11.cloned.1.call-start
  617.8 0.6 copy-done.3
  618.4 362.4 %reduce-scatter.3.cloned.1.call-done = bf16[12,288,2048]{2,1,0:T(8,128)(2,1)} async-done(((bf16[12,1152,2048]{2,1,0:T(8,128)(2,1)}), bf16[12,288,2048]{2,1,0:T(8,128)(2,1)}) %reduce-scatter.3.cloned.1.call-update) | async-done | bytes 14155792 | tf_op jit(solution)/shard_map/reduce_scatter | solution.py:61
  980.8 13.0 fusion.16
  993.8 0.4 copy-done.2
  994.1 15.4 fusion.18
  1009.5 0.0 all-gather.11.cloned.1.call-update
  1009.5 0.0 reduce-scatter.5.cloned.1.call-start
  1009.5 330.9 %all-gather.11.cloned.1.call-done = bf16[12,1152,2048]{2,1,0:T(8,128)(2,1)} async-done(((bf16[12,288,2048]{2,1,0:T(8,128)(2,1)}), bf16[12,1152,2048]{2,1,0:T(8,128)(2,1)}) %all-gather.11.cloned.1.call-update) | async-done | bytes 56623120 | tf_op jit(solution)/shard_map/all_gather | solution.py:64
  1340.4 286.2 %fusion.7 = f32[12,1152,4096]{2,1,0:T(8,128)} fusion(bf16[12,1152,2048]{2,1,0:T(8,128)(2,1)} %all-gather.11.cloned.1.call-done, bf16[2048,4096]{1,0:T(8,128)(2,1)} %param.21), kind=kOutput, calls=%fused_computation.8 | convolution fusion | flops 232381218816 | bytes 299892736 | tf_op jit(solution)/shard_map/bsd,df->bsf/dot_general | solution.py:65
  1626.6 250.0 %multiply_convert_fusion = bf16[12,1152,4096]{2,1,0:T(8,128)(2,1)} fusion(f32[12,1152,4096]{2,1,0:T(8,128)} %fusion.7, bf16[12,1152,2048]{2,1,0:T(8,128)(2,1)} %all-gather.11.cloned.1.call-done, bf16[2048,4096]{1,0:T(8,128)(2,1)} %param.22), kind=kOutput, calls=%fused_computation.9 | convolution fusion | flops 232041480192 | bytes 413138944 | tf_op jit(solution)/shard_map/bsd,df->bsf/dot_general | solution.py:66
  1876.6 247.8 %convolution_convert_fusion = bf16[12,1152,2048]{2,1,0:T(8,128)(2,1)} fusion(bf16[12,1152,4096]{2,1,0:T(8,128)(2,1)} %multiply_convert_fusion, bf16[4096,2048]{1,0:T(8,128)(2,1)} %param.23), kind=kOutput, calls=%fused_computation.18 | convolution fusion | flops 231956545536 | bytes 186646528 | tf_op jit(solution)/shard_map/bsf,fd->bsd/dot_general | solution.py:68
  2124.4 0.0 reduce-scatter.5.cloned.1.call-update
  2124.4 0.0 copy-start.1
  2124.5 363.3 %reduce-scatter.5.cloned.1.call-done = bf16[12,288,2048]{2,1,0:T(8,128)(2,1)} async-done(((bf16[12,1152,2048]{2,1,0:T(8,128)(2,1)}), bf16[12,288,2048]{2,1,0:T(8,128)(2,1)}) %reduce-scatter.5.cloned.1.call-update) | async-done | bytes 14155792 | tf_op jit(solution)/shard_map/reduce_scatter | solution.py:69
  2487.8 21.5 fusion.19
  (12 shorter events, 0.1 us)
Async XLA Ops:
  7.2 524.5 %copy-start = (bf16[512,2048]{1,0:T(8,128)(2,1)S(1)}, bf16[512,2048]{1,0:T(8,128)(2,1)}, u32[]{:S(2)}) copy-start(bf16[512,2048]{1,0:T(8,128)(2,1)} %param.19) | copy-start | bytes 6291460
  7.2 354.8 %all-gather.9.cloned.1.call-start = ((), (), s32[]{:S(2)}) async-start(), calls=%async_computation.4 | async-start | bytes 70778880 | tf_op jit(solution)/shard_map/all_gather | solution.py:49
  29.5 437.8 %all-gather.7.cloned.1.call-start = ((), (), s32[]{:S(2)}) async-start(), calls=%async_computation.3 | async-start | bytes 8847360 | tf_op jit(solution)/shard_map/all_gather | solution.py:50
  39.7 12.5 copy-start.4
  39.8 12.5 copy-start.5
  41.2 490.4 %all-gather.5.cloned.1.call-start = ((), (), s32[]{:S(2)}) async-start(), calls=%async_computation.2 | async-start | bytes 8847360 | tf_op jit(solution)/shard_map/all_gather | solution.py:51
  51.8 928.9 %reduce-scatter.3.cloned.1.call-start = ((), (), s32[]{:S(2)}) async-start(), calls=%async_computation.5 | async-start | bytes 70778880 | tf_op jit(solution)/shard_map/reduce_scatter | solution.py:61
  617.7 0.7 copy-start.3
  617.7 722.7 %all-gather.11.cloned.1.call-start = ((), (), s32[]{:S(2)}) async-start(), calls=%async_computation.6 | async-start | bytes 70778880 | tf_op jit(solution)/shard_map/all_gather | solution.py:64
  980.7 13.4 copy-start.2
  1009.5 1478.3 %reduce-scatter.5.cloned.1.call-start = ((), (), s32[]{:S(2)}) async-start(), calls=%async_computation.7 | async-start | bytes 70778880 | tf_op jit(solution)/shard_map/reduce_scatter | solution.py:69
  2124.4 384.9 %copy-start.1 = (bf16[512,2048]{1,0:T(8,128)(2,1)S(1)}, bf16[512,2048]{1,0:T(8,128)(2,1)}, u32[]{:S(2)}) copy-start(bf16[512,2048]{1,0:T(8,128)(2,1)} %param.19) | copy-start | bytes 6291460
Sparse Core Ops, SparseCore 0:
  29.6 332.3 all-gather.8
  364.1 48.1 all-gather.6
  414.4 48.1 all-gather.4
  617.8 362.8 reduce-scatter.2
  1009.6 330.7 all-gather.10
  2124.6 363.1 reduce-scatter.4
where the time goes:
time: 2530 us; the launch traced here: 2520 us
  waiting for transfers between devices  1350 us (53%)
  matrix products  990 us (39%)
  other arithmetic  107 us (4%)
  local copies, waits for them, and re-layouts  50 us (2%)
    reduce_scatter x1, waiting for transfers between devices, local_layer(): mlp_out = lax.psum_scatter(mlp_part, 'tp', scatter_dimension=1, tiled=True)  363 us
    reduce_scatter x1, waiting for transfers between devices, local_layer(): lax.psum_scatter(attn_part, 'tp', scatter_dimension=1, tiled=True)  362 us
    all_gather x1, waiting for transfers between devices, local_layer(): normed_mlp_full = lax.all_gather(normed_mlp, 'tp', axis=1, tiled=True)  331 us
    all_gather x1, waiting for transfers between devices, local_layer(): normed_full = lax.all_gather(normed, 'tp', axis=1, tiled=True)  298 us
    dot_general x1, matrix products, local_layer(): jnp.einsum('bsd,df->bsf', normed_mlp_full, w_gate, preferred_element_type...  286 us
    dot_general x1, matrix products, local_layer(): jnp.einsum('bsd,df->bsf', normed_mlp_full, w_up, preferred_element_type=j...  250 us
    dot_general x1, matrix products, local_layer(): jnp.einsum('bsf,fd->bsd', mlp_act, w_down, preferred_element_type=jnp.flo...  248 us
    dot_general x1, matrix products, local_layer(): jnp.einsum('crif,ife->cre', attn_vals, w_out.reshape(local_heads, head_di...  86 us
  transfers between devices with their start and end apart: 6, of which 4 were waited for; matrix products, arithmetic and copies ran while one was open for 8% of the time, Pallas kernels for 0%

commit v1 on v0

v1 whole, which is shorter than its diff:
```python
import functools

import jax
import jax.numpy as jnp
import numpy as np
from jax import lax
from jax.experimental import pallas as pl
from jax.experimental.pallas import tpu as pltpu
from jax.sharding import PartitionSpec as P

NORM_EPS = 1e-6
ROPE_BASE = 10000.0
MASK_FILL = -1e30
F32 = jnp.float32
BF16 = jnp.bfloat16
MESH = pl.DeviceIdType.MESH
VMEM_LIMIT = 67043328


def rope_tables(seq, head_dim):
    inv_freq = ROPE_BASE ** (-2.0 * np.arange(head_dim // 2) / head_dim)
    angles = np.arange(seq)[:, None] * inv_freq[None, :]
    return np.cos(angles).astype(np.float32), np.sin(angles).astype(np.float32)


def normalize(rows, gain):
    inv = lax.rsqrt(jnp.mean(rows * rows, axis=-1, keepdims=True) + NORM_EPS)
    return (rows * inv * (1.0 + gain)).astype(BF16)


def dot(a, b):
    return jnp.dot(a, b, preferred_element_type=F32)


def span(index, size):
    return pl.ds(pl.multiple_of(index * size, size), size)


def start(copies):
    for c in copies:
        c.start()


def wait_recv(copies):
    for c in copies:
        c.wait_recv()


def wait_send(copies):
    for c in copies:
        c.wait_send()


def send(src, dst, send_sem, recv_sem, peer):
    return pltpu.make_async_remote_copy(src_ref=src, dst_ref=dst, send_sem=send_sem, recv_sem=recv_sem, device_id=peer, device_id_type=MESH)


def peers():
    dp = lax.axis_index("dp")
    tp = lax.axis_index("tp")
    core_tp = tp + 1 - 2 * lax.rem(tp, 2)
    chip_tp = lax.rem(tp + 2, 4)
    return dp, tp, chip_tp, {"tp": core_tp}, {"tp": chip_tp}, {"dp": 1 - dp}


def enter(*others):
    barrier = pltpu.get_barrier_semaphore()
    for peer in others:
        pl.semaphore_signal(barrier, inc=1, device_id=peer, device_id_type=MESH)
    pl.semaphore_wait(barrier, len(others))


Q_PIECES = 2
O_PIECES = 4


def attention_kernel(plen_ref, vlen_ref, gain_ref, h_hbm, cos_hbm, sin_hbm, wq_hbm, wk_hbm, wv_hbm, wo_hbm,
                     h1_hbm, key_hbm, value_hbm, wo_far,
                     x_v, q_v, kv_v, w_v, wkv_v, cos_v, sin_v,
                     table_sem, x_sem, wkv_sem, w_sem, out_sem, key_sem,
                     qc_send, qc_recv, qx_send, qx_recv, qy_send, qy_recv, qxc_send, qxc_recv, qyc_send, qyc_recv,
                     oc_send, oc_recv, ox_send, ox_recv, oy_send, oy_recv, oxc_send, oxc_recv, oyc_send, oyc_recv,
                     kx_send, kx_recv, kc_send, kc_recv, kxc_send, kxc_recv):
    num_batch, rows, width = x_v.shape
    heads, hd = q_v.shape[1], q_v.shape[3]
    seq = kv_v.shape[1]
    own_heads = wq_hbm.shape[1] // hd
    half = hd // 2
    dp, tp, chip_tp, core_peer, chip_peer, group_peer = peers()
    own_rows = span(tp, rows)
    chip_rows = span(chip_tp, rows)

    tables = [pltpu.make_async_copy(t.at[own_rows], v, table_sem.at[i]) for i, (t, v) in enumerate(((cos_hbm, cos_v), (sin_hbm, sin_v)))]
    wkv = [pltpu.make_async_copy(w, wkv_v.at[i], wkv_sem.at[i]) for i, w in enumerate((wk_hbm, wv_hbm))]
    own_q = [pltpu.make_async_copy(wq_hbm.at[:, pl.ds(i * hd, hd)], w_v.at[i], w_sem.at[i, 0]) for i in range(own_heads)]

    def x_load(s):
        return pltpu.make_async_copy(h_hbm.at[s], x_v.at[s], x_sem.at[s])

    def own_o(n):
        return pltpu.make_async_copy(wo_hbm.at[:, pl.ds(n * hd, hd)], w_v.at[n, pl.ds(0, own_heads * hd)], w_sem.at[n, 0])

    def far_o(n):
        size = (heads - own_heads) * hd
        return pltpu.make_async_copy(wo_far.at[:, pl.ds(n * hd, hd)], w_v.at[n, pl.ds(own_heads * hd, size)], w_sem.at[n, 1])

    q_core = [send(wq_hbm.at[:, pl.ds(i * hd, hd)], w_v.at[own_heads + i], qc_send.at[i], qc_recv.at[i], core_peer) for i in range(own_heads)]
    q_rows = width // Q_PIECES

    def q_chip(i):
        return send(wq_hbm.at[pl.ds(i * q_rows, q_rows), span(dp, hd)], w_v.at[4, pl.ds(i * q_rows, q_rows)], qx_send.at[i], qx_recv.at[i], chip_peer)

    def q_move(src, dst, i, send_sem, recv_sem, peer):
        at = pl.ds(i * q_rows, q_rows)
        return send(w_v.at[src, at], w_v.at[dst, at], send_sem.at[i], recv_sem.at[i], peer)

    def q_group(i):
        return q_move(4, 6, i, qy_send, qy_recv, group_peer)

    def q_chip_core(i):
        return q_move(4, 5, i, qxc_send, qxc_recv, core_peer)

    def q_group_core(i):
        return q_move(6, 7, i, qyc_send, qyc_recv, core_peer)

    own_width = own_heads * hd
    o_rows = hd // O_PIECES
    o_core = [send(wo_hbm, wo_far.at[pl.ds(0, own_width)], oc_send.at[0], oc_recv.at[0], core_peer)]

    def far_rows(slot, i):
        return wo_far.at[pl.ds((slot - own_heads) * hd + i * o_rows, o_rows)]

    def o_chip(i):
        src = wo_hbm.at[pl.ds(pl.multiple_of(dp * hd + i * o_rows, o_rows), o_rows)]
        return send(src, far_rows(4, i), ox_send.at[i], ox_recv.at[i], chip_peer)

    def o_group(i):
        return send(far_rows(4, i), far_rows(6, i), oy_send.at[i], oy_recv.at[i], group_peer)

    def o_chip_core(i):
        return send(far_rows(4, i), far_rows(5, i), oxc_send.at[i], oxc_recv.at[i], core_peer)

    def o_group_core(i):
        return send(far_rows(6, i), far_rows(7, i), oyc_send.at[i], oyc_recv.at[i], core_peer)

    def kv_chip(s):
        return send(kv_v.at[s, own_rows], kv_v.at[s, own_rows], kx_send.at[s], kx_recv.at[s], chip_peer)

    def kv_core(s):
        return send(kv_v.at[s, own_rows], kv_v.at[s, own_rows], kc_send.at[s], kc_recv.at[s], core_peer)

    def kv_chip_core(s):
        return send(kv_v.at[s, chip_rows], kv_v.at[s, chip_rows], kxc_send.at[s], kxc_recv.at[s], core_peer)

    def kv_stores(s):
        outs = ((key_hbm, 0), (value_hbm, hd))
        return [pltpu.make_async_copy(kv_v.at[s, own_rows, pl.ds(at, hd)], ref.at[s], key_sem.at[s, i]) for i, (ref, at) in enumerate(outs)]

    def kv_send(s):
        kv_chip(s).start()
        kv_core(s).start()
        start(kv_stores(s))

    x_load(0).start()
    start(wkv + tables + own_q)

    @pl.loop(1, num_batch)
    def _(s):
        x_load(s).start()

    enter(core_peer, chip_peer, group_peer)
    start([q_chip(i) for i in range(Q_PIECES)])
    start(q_core)
    start([o_chip(i) for i in range(O_PIECES)])
    start(o_core)

    for c in tables + wkv + own_q:
        c.wait()
    gain = gain_ref[...].astype(F32)

    def rope(x, cos, sin):
        a, c = x[:, :half], x[:, half:]
        return a * cos - c * sin, c * cos + a * sin

    def store_query(q, cos, sin, at, slot):
        lo, hi = rope(q, cos, sin)
        shape = q_v[at, slot, :, :half].shape
        q_v[at, slot, :, :half] = lo.astype(BF16).reshape(shape)
        q_v[at, slot, :, half:] = hi.astype(BF16).reshape(shape)

    @pl.loop(0, num_batch)
    def _(s):
        @pl.when(s == 5)
        def _():
            q_chip(0).wait_recv()
            start([q_group(0), q_chip_core(0)])

        @pl.when(s == num_batch - 1)
        def _():
            for i in range(1, Q_PIECES):
                q_chip(i).wait_recv()
                start([q_group(i), q_chip_core(i)])

        @pl.when(s > 0)
        def _():
            kv_send(s - 1)

        x_load(s).wait()
        xn = normalize(x_v[s].astype(F32), gain)
        x_v[s] = xn
        cos, sin = cos_v[...], sin_v[...]
        lo, hi = rope(dot(xn, wkv_v[0]), cos, sin)
        kv_v[s, own_rows, :half] = lo.astype(BF16)
        kv_v[s, own_rows, half:hd] = hi.astype(BF16)
        kv_v[s, own_rows, hd:] = dot(xn, wkv_v[1]).astype(BF16)
        for i in range(own_heads):
            store_query(dot(xn, w_v[i]), cos * hd**-0.5, sin * hd**-0.5, s, i)

    kv_send(num_batch - 1)

    group = 3

    @pl.loop(own_heads, heads)
    def _(slot):
        @pl.when(slot == 2)
        def _():
            wait_recv(q_core)

        @pl.when(slot == 3)
        def _():
            o_chip(0).wait_recv()
            start([o_group(0), o_chip_core(0)])

        @pl.when(slot == 5)
        def _():
            wait_recv([q_chip_core(i) for i in range(Q_PIECES)])
            o_chip(1).wait_recv()
            start([o_group(1), o_chip_core(1)])

        @pl.when(slot == 6)
        def _():
            for i in range(Q_PIECES):
                q_group(i).wait_recv()
                q_group_core(i).start()
            o_chip(2).wait_recv()
            start([o_group(2), o_chip_core(2)])

        @pl.when(slot == 7)
        def _():
            wait_recv([q_group_core(i) for i in range(Q_PIECES)])
            o_chip(3).wait_recv()
            start([o_group(3), o_chip_core(3)])

        @pl.loop(0, num_batch // group)
        def _(i):
            at = span(i, group)
            cos = jnp.concatenate([cos_v[...] * hd**-0.5] * group, axis=0)
            sin = jnp.concatenate([sin_v[...] * hd**-0.5] * group, axis=0)
            store_query(dot(x_v[at].reshape(group * rows, width), w_v[slot]), cos, sin, at, slot)

    for copies in ([q_group(i) for i in range(Q_PIECES)], [q_chip_core(i) for i in range(Q_PIECES)], [q_group_core(i) for i in range(Q_PIECES)]):
        wait_send(copies)
    for n in range(heads):
        own_o(n).start()

    @pl.loop(0, num_batch)
    def _(s):
        x_load(s).start()

    kv_chip(0).wait_recv()
    kv_chip_core(0).start()
    for i in range(O_PIECES):
        o_group(i).wait_recv()
        o_group_core(i).start()
    wait_recv(o_core + [o_chip_core(i) for i in range(O_PIECES)] + [o_group_core(i) for i in range(O_PIECES)])
    for n in range(heads):
        far_o(n).start()

    tail = 128
    col = lax.broadcasted_iota(jnp.int32, (rows, tail), 1) + (seq - tail)
    row = lax.broadcasted_iota(jnp.int32, (rows, tail), 0) + tp * rows

    def score(s, p):
        return lax.dot_general(q_v[s, p], kv_v[s, :, :hd], (((1,), (1,)), ((), ())), preferred_element_type=F32)

    def probs(sc, allowed):
        sc = jnp.concatenate([sc[:, : seq - tail], jnp.where(allowed, sc[:, seq - tail :], MASK_FILL)], axis=1)
        p = jnp.exp(sc - jnp.max(sc, axis=-1, keepdims=True))
        return (p * (1.0 / jnp.sum(p, axis=-1, keepdims=True))).astype(BF16)

    def project(s, n):
        o = jnp.concatenate([q_v[s, j] for j in range(heads)], axis=1)
        at = slice(n * hd, (n + 1) * hd)
        x_v[s, :, at] = (x_v[s, :, at].astype(F32) + dot(o, w_v[n]).astype(BF16).astype(F32)).astype(BF16)

    def out_store(s):
        return pltpu.make_async_copy(x_v.at[s], h1_hbm.at[s], out_sem.at[s])

    def attend(s, project_too):
        wait_recv([kv_core(s), kv_chip_core(s)])
        allowed = (col < vlen_ref[s]) & ((col < plen_ref[s]) | (col <= row))
        if project_too:
            x_load(s - 1).wait()
        for first in (0, heads // 2):
            if first:

                @pl.when(s < num_batch - 1)
                def _():
                    kv_chip(s + 1).wait_recv()
                    kv_chip_core(s + 1).start()

            sc = score(s, first)
            for p in range(first, first + heads // 2):
                ahead = score(s, p + 1) if p + 1 < first + heads // 2 else None
                if project_too:
                    project(s - 1, p)
                q_v[s, p] = dot(probs(sc, allowed), kv_v[s, :, hd:]).astype(BF16)
                sc = ahead
        if project_too:
            out_store(s - 1).start()

    attend(0, False)
    for n in range(heads):
        own_o(n).wait()
        far_o(n).wait()

    @pl.loop(1, num_batch)
    def _(s):
        attend(s, True)

    x_load(num_batch - 1).wait()
    for n in range(heads):
        project(num_batch - 1, n)
    out_store(num_batch - 1).start()

    wait_send(q_core + o_core + [q_chip(i) for i in range(Q_PIECES)])
    for i in range(O_PIECES):
        wait_send([o_chip(i), o_group(i), o_chip_core(i), o_group_core(i)])

    @pl.loop(0, num_batch)
    def _(s):
        wait_send([kv_chip(s), kv_core(s), kv_chip_core(s)])
        for c in kv_stores(s):
            c.wait()
        out_store(s).wait()


def attention(hidden, prefix_len, valid_len, norm_attn, w_query, w_key, w_value, w_out, tp_size):
    num_batch, rows, width = hidden.shape
    hd = w_key.shape[1]
    own_heads = w_query.shape[1] // hd
    heads = own_heads * tp_size
    seq = rows * tp_size
    cos, sin = rope_tables(seq, hd)
    any_spec = pl.BlockSpec(memory_space=pl.ANY)
    smem = pl.BlockSpec(memory_space=pltpu.SMEM)
    dma = pltpu.SemaphoreType.DMA
    shape = jax.ShapeDtypeStruct
    flops = 2 * num_batch * rows * (width * (2 * heads + 2) * hd + 2 * heads * hd * seq)
    out = pl.pallas_call(
        attention_kernel,
        in_specs=[smem, smem, pl.BlockSpec(memory_space=pltpu.VMEM)] + [any_spec] * 7,
        out_specs=[any_spec] * 4,
        out_shape=[
            shape((num_batch, rows, width), BF16),
            shape((num_batch, rows, hd), BF16),
            shape((num_batch, rows, hd), BF16),
            shape(((heads - own_heads) * hd, width), BF16),
        ],
        scratch_shapes=[
            pltpu.VMEM((num_batch, rows, width), BF16),
            pltpu.VMEM((num_batch, heads, rows, hd), BF16),
            pltpu.VMEM((num_batch, seq, 2 * hd), BF16),
            pltpu.VMEM((heads, width, hd), BF16),
            pltpu.VMEM((2, width, hd), BF16),
            pltpu.VMEM((rows, hd // 2), F32),
            pltpu.VMEM((rows, hd // 2), F32),
            dma((2,)),
            dma((num_batch,)),
            dma((2,)),
            dma((heads, 2)),
            dma((num_batch,)),
            dma((num_batch, 2)),
        ]
        + [dma((own_heads,))] * 2
        + [dma((Q_PIECES,))] * 8
        + [dma((1,))] * 2
        + [dma((O_PIECES,))] * 8
        + [dma((num_batch,))] * 6,
        compiler_params=pltpu.CompilerParams(vmem_limit_bytes=VMEM_LIMIT, collective_id=1, has_side_effects=True),
        cost_estimate=pl.CostEstimate(flops=flops, bytes_accessed=num_batch * rows * width * 6, transcendentals=num_batch * rows * heads * seq),
        name="attention",
    )(prefix_len, valid_len, norm_attn.reshape(1, width), hidden, jnp.asarray(cos), jnp.asarray(sin), w_query, w_key, w_value, w_out)
    return out[:3]


def mlp_kernel(gain_ref, h_hbm, wg_hbm, wu_hbm, wd_hbm, out_hbm, pg_hbm, pu_hbm, pd_hbm, rg_hbm, ru_hbm, rd_hbm,
               x_v, acc_v, act_v, wg_v, wu_v, wd_v, load_sem, x_sem, out_sem,
               p_send, p_recv, a_send, a_recv, ac_send, ac_recv, b_send, b_recv, bc_send, bc_recv):
    rows, width = x_v.shape
    tile = act_v.shape[0]
    tiles = rows // tile
    unit = wg_v.shape[2]
    piece = unit // 2
    own = wg_hbm.shape[1] // unit
    pieces = own // 2 * 2
    groups, per_group = rg_hbm.shape[:2]
    steps = 2 * own + groups * per_group
    dp, tp, chip_tp, core_peer, chip_peer, group_peer = peers()

    def piece_refs(group, j):
        at = pl.ds(pl.multiple_of(lax.rem(j, 2) * piece, piece), piece)
        return rg_hbm.at[group, j // 2, :, at], ru_hbm.at[group, j // 2, :, at], rd_hbm.at[group, j // 2, at, :]

    def own_copies():
        refs = ((wg_hbm, pg_hbm), (wu_hbm, pu_hbm), (wd_hbm, pd_hbm))
        return [send(src, dst, p_send.at[i], p_recv.at[i], core_peer) for i, (src, dst) in enumerate(refs)]

    def chip_copies(j):
        at = pl.ds(pl.multiple_of(dp * pieces * piece + j * piece, piece), piece)
        src = (wg_hbm.at[:, at], wu_hbm.at[:, at], wd_hbm.at[at, :])
        return [send(s, d, a_send.at[j, i], a_recv.at[j, i], chip_peer) for i, (s, d) in enumerate(zip(src, piece_refs(0, j)))]

    def relay(j, source, target, send_sems, recv_sems, peer):
        pairs = zip(piece_refs(source, j), piece_refs(target, j))
        return [send(s, d, send_sems.at[j, i], recv_sems.at[j, i], peer) for i, (s, d) in enumerate(pairs)]

    def core_a(j):
        return relay(j, 0, 1, ac_send, ac_recv, core_peer)

    def group_a(j):
        return relay(j, 0, 2, b_send, b_recv, group_peer)

    def core_b(j):
        return relay(j, 2, 3, bc_send, bc_recv, core_peer)

    def h_copy(m):
        at = span(m, tile)
        return pltpu.make_async_copy(h_hbm.at[at], x_v.at[at], x_sem.at[m])

    def load(src, slot):
        return [pltpu.make_async_copy(s, d.at[slot], load_sem.at[slot, i]) for i, (s, d) in enumerate(zip(src, (wg_v, wu_v, wd_v)))]

    def own_load(u, slot):
        at = pl.ds(pl.multiple_of(u * unit, unit), unit)
        return load((wg_hbm.at[:, at], wu_hbm.at[:, at], wd_hbm.at[at, :]), slot)

    def peer_load(u, slot):
        at = pl.ds(pl.multiple_of((u - own) * unit, unit), unit)
        return load((pg_hbm.at[:, at], pu_hbm.at[:, at], pd_hbm.at[at, :]), slot)

    def far_load(u, slot):
        i = u - 2 * own
        g = lax.rem(i, groups)
        p = i // groups
        return load((rg_hbm.at[g, p], ru_hbm.at[g, p], rd_hbm.at[g, p]), slot)

    for m in range(tiles):
        h_copy(m).start()
    start(own_load(0, 0))
    enter(core_peer, chip_peer, group_peer)
    start(own_copies())

    @pl.loop(0, pieces)
    def _(j):
        start(chip_copies(j))

    acc_v[...] = jnp.zeros_like(acc_v)
    gain = gain_ref[...].astype(F32)
    for m in range(tiles):
        h_copy(m).wait()

        @pl.loop(0, tile // 96)
        def _(i):
            at = span(m * (tile // 96) + i, 96)
            x_v[at, :] = normalize(x_v[at, :].astype(F32), gain)

    def out_copy(m):
        at = pl.ds(pl.multiple_of(m * tile, tile), tile)
        return pltpu.make_async_copy(x_v.at[at], out_hbm.at[at], out_sem.at[m])

    def finish(m):
        h_copy(m).wait()
        chunk = 48

        @pl.loop(0, tile // chunk)
        def _(i):
            at = pl.ds(pl.multiple_of(m * tile + i * chunk, chunk), chunk)
            x_v[at, :] = (x_v[at, :].astype(F32) + acc_v[at, :].astype(BF16).astype(F32)).astype(BF16)

        out_copy(m).start()

    first_a, first_b, every = 4, 8, 3

    @pl.loop(0, steps)
    def _(s):
        slot = lax.rem(s, 2)

        @pl.when((s >= first_a) & (s < first_a + every * pieces) & (lax.rem(s - first_a + every, every) == 0))
        def _():
            j = (s - first_a) // every
            wait_recv(chip_copies(j))
            start(group_a(j))
            start(core_a(j))

        @pl.when((s >= first_b) & (s < first_b + every * pieces) & (lax.rem(s - first_b + 2 * every, every) == 0))
        def _():
            j = (s - first_b) // every
            wait_recv(group_a(j))
            start(core_b(j))

        u = s + 1

        @pl.when(u < own)
        def _():
            start(own_load(u, 1 - slot))

        @pl.when(u == own)
        def _():
            wait_recv(own_copies())

        @pl.when((u >= own) & (u < 2 * own))
        def _():
            start(peer_load(u, 1 - slot))

        @pl.when((u >= 2 * own) & (u < steps))
        def _():
            g = lax.rem(u - 2 * own, groups)
            p = (u - 2 * own) // groups

            @pl.when(g == 1)
            def _():
                for j in (2 * p, 2 * p + 1):
                    wait_recv(core_a(j))

            @pl.when(g == 3)
            def _():
                for j in (2 * p, 2 * p + 1):
                    wait_recv(core_b(j))

            start(far_load(u, 1 - slot))

        for c in own_load(0, slot):
            c.wait()

        @pl.loop(0, tiles)
        def _(m):
            at = pl.ds(pl.multiple_of(m * tile, tile), tile)
            gate = dot(x_v[at, :], wg_v[slot])
            up = dot(x_v[at, :], wu_v[slot])
            act_v[...] = (jax.nn.gelu(gate, approximate=True) * up).astype(BF16)
            for n in range(0, width, unit):
                acc_v[at, n : n + unit] += dot(act_v[...], wd_v[slot, :, n : n + unit])

            @pl.when(s == steps - 1)
            def _():
                h_copy(m).start()

                @pl.when(m > 0)
                def _():
                    finish(m - 1)

    finish(tiles - 1)
    wait_send(own_copies())

    @pl.loop(0, pieces)
    def _(j):
        for copies in (chip_copies(j), group_a(j), core_a(j), core_b(j)):
            wait_send(copies)

    for m in range(tiles):
        out_copy(m).wait()


def mlp(h1, norm_mlp, w_gate, w_up, w_down):
    rows, width = h1.shape
    ff = w_gate.shape[1]
    unit = 512
    tile = rows // 3
    far = ff // 2 // unit
    pieces = 2 * far
    shapes = [(rows, width), (width, ff), (width, ff), (ff, width), (4, far, width, unit), (4, far, width, unit), (4, far, unit, width)]
    any_spec = pl.BlockSpec(memory_space=pl.ANY)
    dma = pltpu.SemaphoreType.DMA
    out = pl.pallas_call(
        mlp_kernel,
        in_specs=[pl.BlockSpec(memory_space=pltpu.VMEM)] + [any_spec] * 4,
        out_specs=[any_spec] * 7,
        out_shape=[jax.ShapeDtypeStruct(s, BF16) for s in shapes],
        scratch_shapes=[
            pltpu.VMEM((rows, width), BF16),
            pltpu.VMEM((rows, width), F32),
            pltpu.VMEM((tile, unit), BF16),
            pltpu.VMEM((2, width, unit), BF16),
            pltpu.VMEM((2, width, unit), BF16),
            pltpu.VMEM((2, unit, width), BF16),
            dma((2, 3)),
            dma((rows // tile,)),
            dma((rows // tile,)),
            dma((3,)),
            dma((3,)),
        ]
        + [dma((pieces, 3))] * 8,
        compiler_params=pltpu.CompilerParams(vmem_limit_bytes=VMEM_LIMIT, collective_id=0, has_side_effects=True),
        cost_estimate=pl.CostEstimate(flops=2 * rows * width * ff * 3 * 4, bytes_accessed=4 * 3 * width * ff * 2, transcendentals=0),
        name="mlp",
    )(norm_mlp.reshape(1, width), h1, w_gate, w_up, w_down)
    return out[0]


def solution(mesh):
    tp_size = mesh.shape["tp"]
    row_spec = P("dp", "tp", None)
    arg_specs = (row_spec, P("dp"), P("dp"), P(), P(None, "tp"), P(), P(), P("tp", None), P(), P(None, "tp"), P(None, "tp"), P("tp", None))

    def local_layer(hidden, prefix_len, valid_len, norm_attn, w_query, w_key, w_value, w_out, norm_mlp, w_gate, w_up, w_down):
        h1, key, value = attention(hidden, prefix_len, valid_len, norm_attn, w_query, w_key, w_value, w_out, tp_size)
        out = mlp(h1.reshape(-1, hidden.shape[-1]), norm_mlp, w_gate, w_up, w_down)
        return out.reshape(hidden.shape), key, value

    return jax.shard_map(local_layer, mesh=mesh, in_specs=arg_specs, out_specs=(row_spec, row_spec, row_spec), check_vma=False)
```

time: 2530 us -> 916 us (0.36)
  waiting for transfers between devices: 1350 us -> 0 us
  matrix products: 990 us -> 0 us
  Pallas kernels: 0 us -> 898 us
  other arithmetic: 107 us -> 0 us
  local copies, waits for them, and re-layouts: 50 us -> 16.8 us
    dot_general x7 -> x0, matrix products: 926 us -> none  [the longest x1 286 us: local_layer(): jnp.einsum('bsd,df->bsf', normed_mlp_full, w_gate, preferred_element_type...]
    pallas_call x0 -> x2, Pallas kernels: none -> 898 us  [the longest x1 751 us: mlp(): pl.pallas_call(mlp_kernel, in_specs=[pl.BlockSpec(memory_space=pltpu.VMEM...]
    reduce_scatter x2 -> x0, waiting for transfers between devices: 726 us -> none  [the longest x1 363 us: local_layer(): mlp_out = lax.psum_scatter(mlp_part, 'tp', scatter_dimension=1, tiled=True)]
    all_gather x4 -> x0, waiting for transfers between devices: 629 us -> none  [the longest x1 331 us: local_layer(): normed_mlp_full = lax.all_gather(normed_mlp, 'tp', axis=1, tiled=True)]
    sub x1 -> x0, matrix products: 64.3 us -> none  [local_layer(): jax.nn.softmax(jnp.where(allowed[:, None], scores, MASK_FILL), axis=-1)]
    convert_element_type x4 -> x0, other arithmetic: 50.4 us -> none  [the longest x2 28.9 us: rms_norm(): (acts_f32 * inv_rms * (1.0 + norm_scale.astype(jnp.float32))).astype(jnp....]
  transfers between devices with their start and end apart: 6 -> 0, of which waited for: 4 -> 0; matrix products, arithmetic and copies ran while one was open for 8% -> 0% of each run, Pallas kernels for 0% -> 0%
where the time goes in v1:
time: 916 us; the launch traced here: 915 us
  Pallas kernels  898 us (98%)
  local copies, waits for them, and re-layouts  16.8 us (2%)
    pallas_call x1, Pallas kernels, mlp(): pl.pallas_call(mlp_kernel, in_specs=[pl.BlockSpec(memory_space=pltpu.VMEM...  751 us
    pallas_call x1, Pallas kernels, attention(): pl.pallas_call(attention_kernel, in_specs=[smem, smem, pl.BlockSpec(memor...  147 us

profile of v1, /device:TPU:1, one launch (start us, length us, event | category | flops | bytes accessed | tf_op | source)
XLA Modules:
  0.0 915.5 jit_solution(4897397754694639042)
XLA Ops:
  0.6 1.3 reshape.19.gain_ref
  1.9 1.3 reshape.18.gain_ref
  3.2 147.2 %attention.1 = (bf16[12,288,2048]{2,1,0:T(8,128)(2,1)}, bf16[12,288,256]{2,1,0:T(8,128)(2,1)}, bf16[12,288,256]{2,1,0:T(8,128)(2,1)}, bf16[1536,2048]{1,0:T(8,128)(2,1)}) custom-call(s32[12]{0:T(128)} %plen_ref.1, s32[12]{0:T(128)} %vlen_ref.1, bf16[1,2048]{1,0:T(2,128)(2,1)} %reshape.19.gain_ref, bf16[12,288,2048]{2,1,0:T(8,128)(2,1)} %h_hbm.1, ...), custom_call_target="tpu_custom_call" | custom-call | flops 97844723712 | bytes 42467328 | tf_op jit(solution)/shard_map/attention/pallas_call | solution.py:360
  150.4 750.7 %mlp.1 = (bf16[3456,2048]{1,0:T(8,128)(2,1)}, bf16[2048,4096]{1,0:T(8,128)(2,1)}, bf16[2048,4096]{1,0:T(8,128)(2,1)}, bf16[4096,2048]{1,0:T(8,128)(2,1)}, bf16[4...) custom-call(bf16[1,2048]{1,0:T(2,128)(2,1)} %reshape.18.gain_ref, ...), custom_call_target="tpu_custom_call" | custom-call | flops 695784701952 | bytes 201326592 | tf_op jit(solution)/shard_map/mlp/pallas_call | solution.py:585
  901.2 0.0 copy-start.1
  901.2 0.0 copy-start
  901.2 11.8 %copy.20 = bf16[12,288,2048]{2,1,0:T(8,128)(2,1)} copy(bf16[12,288,2048]{2,1,0:T(8,128)(2,1)} %bitcast.2) | data formatting | bytes 28311552
  913.0 0.0 copy-done.1
  913.0 1.2 copy.21
  914.3 0.0 copy-done
  914.3 1.2 copy.22
Async XLA Ops:
  901.2 11.9 %copy-start.1 = (bf16[12,288,256]{2,1,0:T(8,128)(2,1)S(1)}, bf16[12,288,256]{2,1,0:T(8,128)(2,1)}, u32[]{:S(2)}) copy-start(bf16[12,288,256]{2,1,0:T(8,128)(2,1)} %get-tuple-element.15) | copy-start | bytes 5308420
  901.2 13.1 %copy-start = (bf16[12,288,256]{2,1,0:T(8,128)(2,1)S(1)}, bf16[12,288,256]{2,1,0:T(8,128)(2,1)}, u32[]{:S(2)}) copy-start(bf16[12,288,256]{2,1,0:T(8,128)(2,1)} %get-tuple-element.16) | copy-start | bytes 5308420

commit v2 on v1

--- a/solution.py
+++ b/solution.py
@@ -17,10 +17,11 @@
 VMEM_LIMIT = 67043328
 
 
-def rope_tables(seq, head_dim):
+def rope_tables(rows, blocks, head_dim):
     inv_freq = ROPE_BASE ** (-2.0 * np.arange(head_dim // 2) / head_dim)
-    angles = np.arange(seq)[:, None] * inv_freq[None, :]
-    return np.cos(angles).astype(np.float32), np.sin(angles).astype(np.float32)
+    angles = np.arange(rows)[:, None] * inv_freq[None, :]
+    starts = np.arange(blocks)[:, None] * rows * inv_freq[None, :]
+    return tuple(f(a).astype(np.float32) for a in (angles, starts) for f in (np.cos, np.sin))
 
 
 def normalize(rows, gain):
@@ -74,10 +75,10 @@
 O_PIECES = 4
 
 
-def attention_kernel(plen_ref, vlen_ref, gain_ref, h_hbm, cos_hbm, sin_hbm, wq_hbm, wk_hbm, wv_hbm, wo_hbm,
-                     h1_hbm, key_hbm, value_hbm, wo_far,
-                     x_v, q_v, kv_v, w_v, wkv_v, cos_v, sin_v,
-                     table_sem, x_sem, wkv_sem, w_sem, out_sem, key_sem,
+def attention_kernel(plen_ref, vlen_ref, gain_ref, gain2_ref, h_hbm, cos_ref, sin_ref, cos0_ref, sin0_ref, wq_hbm, wk_hbm, wv_hbm, wo_hbm,
+                     h1_hbm, x2_hbm, key_hbm, value_hbm, wo_far,
+                     x_v, q_v, kv_v, w_v, wkv_v, cos_v, sin_v, x2_v,
+                     x_sem, wkv_sem, w_sem, out_sem, x2_sem, key_sem,
                      qc_send, qc_recv, qx_send, qx_recv, qy_send, qy_recv, qxc_send, qxc_recv, qyc_send, qyc_recv,
                      oc_send, oc_recv, ox_send, ox_recv, oy_send, oy_recv, oxc_send, oxc_recv, oyc_send, oyc_recv,
                      kx_send, kx_recv, kc_send, kc_recv, kxc_send, kxc_recv):
@@ -90,7 +91,6 @@
     own_rows = span(tp, rows)
     chip_rows = span(chip_tp, rows)
 
-    tables = [pltpu.make_async_copy(t.at[own_rows], v, table_sem.at[i]) for i, (t, v) in enumerate(((cos_hbm, cos_v), (sin_hbm, sin_v)))]
     wkv = [pltpu.make_async_copy(w, wkv_v.at[i], wkv_sem.at[i]) for i, w in enumerate((wk_hbm, wv_hbm))]
     own_q = [pltpu.make_async_copy(wq_hbm.at[:, pl.ds(i * hd, hd)], w_v.at[i], w_sem.at[i, 0]) for i in range(own_heads)]
 
@@ -162,7 +162,7 @@
         start(kv_stores(s))
 
     x_load(0).start()
-    start(wkv + tables + own_q)
+    start(wkv + own_q)
 
     @pl.loop(1, num_batch)
     def _(s):
@@ -174,9 +174,12 @@
     start([o_chip(i) for i in range(O_PIECES)])
     start(o_core)
 
-    for c in tables + wkv + own_q:
+    gain = gain_ref[...].astype(F32)
+    cos0, sin0 = cos0_ref[pl.ds(tp, 1), :], sin0_ref[pl.ds(tp, 1), :]
+    cos_v[...] = cos_ref[...] * cos0 - sin_ref[...] * sin0
+    sin_v[...] = sin_ref[...] * cos0 + cos_ref[...] * sin0
+    for c in wkv + own_q:
         c.wait()
-    gain = gain_ref[...].astype(F32)
 
     def rope(x, cos, sin):
         a, c = x[:, :half], x[:, half:]
@@ -290,48 +293,78 @@
 
     def project(s, n):
         o = jnp.concatenate([q_v[s, j] for j in range(heads)], axis=1)
-        at = slice(n * hd, (n + 1) * hd)
+        at = span(n, hd)
         x_v[s, :, at] = (x_v[s, :, at].astype(F32) + dot(o, w_v[n]).astype(BF16).astype(F32)).astype(BF16)
 
-    def out_store(s):
+    gain2 = gain2_ref[...].astype(F32)
+
+    def norm_rows(s, slot, at):
+        x2_v[slot, at, :] = normalize(x_v[s, at, :].astype(F32), gain2)
+
+    def h1_store(s):
         return pltpu.make_async_copy(x_v.at[s], h1_hbm.at[s], out_sem.at[s])
 
-    def attend(s, project_too):
-        wait_recv([kv_core(s), kv_chip_core(s)])
-        allowed = (col < vlen_ref[s]) & ((col < plen_ref[s]) | (col <= row))
-        if project_too:
-            x_load(s - 1).wait()
-        for first in (0, heads // 2):
-            if first:
-
-                @pl.when(s < num_batch - 1)
-                def _():
-                    kv_chip(s + 1).wait_recv()
-                    kv_chip_core(s + 1).start()
-
-            sc = score(s, first)
-            for p in range(first, first + heads // 2):
-                ahead = score(s, p + 1) if p + 1 < first + heads // 2 else None
-                if project_too:
-                    project(s - 1, p)
-                q_v[s, p] = dot(probs(sc, allowed), kv_v[s, :, hd:]).astype(BF16)
-                sc = ahead
-        if project_too:
-            out_store(s - 1).start()
-
-    attend(0, False)
+    def x2_store(s, slot):
+        return pltpu.make_async_copy(x2_v.at[slot], x2_hbm.at[s], x2_sem.at[slot])
+
+    @pl.loop(0, num_batch)
+    def _(s):
+        x_load(s).wait()
+
     for n in range(heads):
         own_o(n).wait()
         far_o(n).wait()
 
-    @pl.loop(1, num_batch)
+    last = num_batch - 1
+
+    @pl.loop(0, num_batch)
     def _(s):
-        attend(s, True)
-
-    x_load(num_batch - 1).wait()
+        before = lax.rem(s + last, num_batch)
+        earlier = lax.rem(s + last - 1, num_batch)
+        slot = lax.rem(s, 2)
+        @pl.when(s < last)
+        def _():
+            kv_chip(s + 1).wait_recv()
+            kv_chip_core(s + 1).start()
+
+        wait_recv([kv_core(s), kv_chip_core(s)])
+        allowed = (col < vlen_ref[s]) & ((col < plen_ref[s]) | (col <= row))
+
+        @pl.when(s >= 4)
+        def _():
+            x2_store(s - 4, slot).wait()
+
+        sc = score(s, 0)
+        for p in range(heads):
+            ahead = score(s, p + 1) if p + 1 < heads else None
+            project(before, p)
+            if p < 6:
+                norm_rows(earlier, slot, pl.ds(p * 48, 48))
+            pr = probs(sc, allowed)
+            q_v[s, p] = dot(pr, kv_v[s, :, hd:]).astype(BF16)
+            sc = ahead
+
+        @pl.when(s >= 1)
+        def _():
+            h1_store(s - 1).start()
+
+        @pl.when(s >= 2)
+        def _():
+            x2_store(s - 2, slot).start()
+
+        @pl.when(s == 1)
+        def _():
+            x_load(last).start()
+
+    x_load(last).wait()
     for n in range(heads):
-        project(num_batch - 1, n)
-    out_store(num_batch - 1).start()
+        project(last, n)
+    h1_store(last).start()
+    for s in (last - 1, last):
+        slot = s % 2
+        x2_store(s - 2, slot).wait()
+        norm_rows(s, slot, slice(None))
+        x2_store(s, slot).start()
 
     wait_send(q_core + o_core + [q_chip(i) for i in range(Q_PIECES)])
     for i in range(O_PIECES):
@@ -342,26 +375,31 @@
         wait_send([kv_chip(s), kv_core(s), kv_chip_core(s)])
         for c in kv_stores(s):
             c.wait()
-        out_store(s).wait()
-
-
-def attention(hidden, prefix_len, valid_len, norm_attn, w_query, w_key, w_value, w_out, tp_size):
+        h1_store(s).wait()
+
+    for s in (last - 1, last):
+        x2_store(s, s % 2).wait()
+
+
+def attention(hidden, prefix_len, valid_len, norm_attn, norm_mlp, w_query, w_key, w_value, w_out, tp_size):
     num_batch, rows, width = hidden.shape
     hd = w_key.shape[1]
     own_heads = w_query.shape[1] // hd
     heads = own_heads * tp_size
     seq = rows * tp_size
-    cos, sin = rope_tables(seq, hd)
+    tables = rope_tables(rows, tp_size, hd)
     any_spec = pl.BlockSpec(memory_space=pl.ANY)
     smem = pl.BlockSpec(memory_space=pltpu.SMEM)
+    vmem = pl.BlockSpec(memory_space=pltpu.VMEM)
     dma = pltpu.SemaphoreType.DMA
     shape = jax.ShapeDtypeStruct
     flops = 2 * num_batch * rows * (width * (2 * heads + 2) * hd + 2 * heads * hd * seq)
     out = pl.pallas_call(
         attention_kernel,
-        in_specs=[smem, smem, pl.BlockSpec(memory_space=pltpu.VMEM)] + [any_spec] * 7,
-        out_specs=[any_spec] * 4,
+        in_specs=[smem, smem, vmem, vmem, any_spec, vmem, vmem, vmem, vmem] + [any_spec] * 4,
+        out_specs=[any_spec] * 5,
         out_shape=[
+            shape((num_batch, rows, width), BF16),
             shape((num_batch, rows, width), BF16),
             shape((num_batch, rows, hd), BF16),
             shape((num_batch, rows, hd), BF16),
@@ -375,11 +413,12 @@
             pltpu.VMEM((2, width, hd), BF16),
             pltpu.VMEM((rows, hd // 2), F32),
             pltpu.VMEM((rows, hd // 2), F32),
-            dma((2,)),
+            pltpu.VMEM((2, rows, width), BF16),
             dma((num_batch,)),
             dma((2,)),
             dma((heads, 2)),
             dma((num_batch,)),
+            dma((2,)),
             dma((num_batch, 2)),
         ]
         + [dma((own_heads,))] * 2
@@ -390,22 +429,36 @@
         compiler_params=pltpu.CompilerParams(vmem_limit_bytes=VMEM_LIMIT, collective_id=1, has_side_effects=True),
         cost_estimate=pl.CostEstimate(flops=flops, bytes_accessed=num_batch * rows * width * 6, transcendentals=num_batch * rows * heads * seq),
         name="attention",
-    )(prefix_len, valid_len, norm_attn.reshape(1, width), hidden, jnp.asarray(cos), jnp.asarray(sin), w_query, w_key, w_value, w_out)
-    return out[:3]
-
-
-def mlp_kernel(gain_ref, h_hbm, wg_hbm, wu_hbm, wd_hbm, out_hbm, pg_hbm, pu_hbm, pd_hbm, rg_hbm, ru_hbm, rd_hbm,
+    )(prefix_len, valid_len, norm_attn, norm_mlp, hidden, *(jnp.asarray(t) for t in tables), w_query, w_key, w_value, w_out)
+    return out[:4]
+
+
+GELU_LINEAR = 0.7978845608028654
+GELU_CUBIC = GELU_LINEAR * 0.044715
+
+
+def expand(x_ref, wg_ref, wu_ref, act_ref):
+    block = 256
+    for n in range(0, act_ref.shape[1], block):
+        at = slice(n, n + block)
+        gate = dot(x_ref[...], wg_ref[:, at])
+        up = dot(x_ref[...], wu_ref[:, at])
+        t = jnp.tanh(gate * (GELU_CUBIC * (gate * gate) + GELU_LINEAR))
+        act_ref[:, at] = ((0.5 * gate) * up * (1.0 + t)).astype(BF16)
+
+
+def mlp_kernel(x_hbm, wg_hbm, wu_hbm, wd_hbm, out_hbm, pg_hbm, pu_hbm, pd_hbm, rg_hbm, ru_hbm, rd_hbm,
                x_v, acc_v, act_v, wg_v, wu_v, wd_v, load_sem, x_sem, out_sem,
                p_send, p_recv, a_send, a_recv, ac_send, ac_recv, b_send, b_recv, bc_send, bc_recv):
     rows, width = x_v.shape
-    tile = act_v.shape[0]
+    tile = act_v.shape[1]
     tiles = rows // tile
     unit = wg_v.shape[2]
     piece = unit // 2
     own = wg_hbm.shape[1] // unit
     pieces = own // 2 * 2
     groups, per_group = rg_hbm.shape[:2]
-    steps = 2 * own + groups * per_group
+    steps = 2 * own + groups * per_group - 1
     dp, tp, chip_tp, core_peer, chip_peer, group_peer = peers()
 
     def piece_refs(group, j):
@@ -434,9 +487,9 @@
     def core_b(j):
         return relay(j, 2, 3, bc_send, bc_recv, core_peer)
 
-    def h_copy(m):
+    def x_copy(m):
         at = span(m, tile)
-        return pltpu.make_async_copy(h_hbm.at[at], x_v.at[at], x_sem.at[m])
+        return pltpu.make_async_copy(x_hbm.at[at], x_v.at[at], x_sem.at[m])
 
     def load(src, slot):
         return [pltpu.make_async_copy(s, d.at[slot], load_sem.at[slot, i]) for i, (s, d) in enumerate(zip(src, (wg_v, wu_v, wd_v)))]
@@ -456,7 +509,7 @@
         return load((rg_hbm.at[g, p], ru_hbm.at[g, p], rd_hbm.at[g, p]), slot)
 
     for m in range(tiles):
-        h_copy(m).start()
+        x_copy(m).start()
     start(own_load(0, 0))
     enter(core_peer, chip_peer, group_peer)
     start(own_copies())
@@ -465,30 +518,16 @@
     def _(j):
         start(chip_copies(j))
 
-    acc_v[...] = jnp.zeros_like(acc_v)
-    gain = gain_ref[...].astype(F32)
+    @pl.loop(0, rows // 96)
+    def _(i):
+        acc_v[span(i, 96), :] = jnp.zeros((96, width), F32)
+
     for m in range(tiles):
-        h_copy(m).wait()
-
-        @pl.loop(0, tile // 96)
-        def _(i):
-            at = span(m * (tile // 96) + i, 96)
-            x_v[at, :] = normalize(x_v[at, :].astype(F32), gain)
+        x_copy(m).wait()
 
     def out_copy(m):
-        at = pl.ds(pl.multiple_of(m * tile, tile), tile)
+        at = span(m, tile)
         return pltpu.make_async_copy(x_v.at[at], out_hbm.at[at], out_sem.at[m])
-
-    def finish(m):
-        h_copy(m).wait()
-        chunk = 48
-
-        @pl.loop(0, tile // chunk)
-        def _(i):
-            at = pl.ds(pl.multiple_of(m * tile + i * chunk, chunk), chunk)
-            x_v[at, :] = (x_v[at, :].astype(F32) + acc_v[at, :].astype(BF16).astype(F32)).astype(BF16)
-
-        out_copy(m).start()
 
     first_a, first_b, every = 4, 8, 3
 
@@ -543,24 +582,23 @@
         for c in own_load(0, slot):
             c.wait()
 
-        @pl.loop(0, tiles)
-        def _(m):
-            at = pl.ds(pl.multiple_of(m * tile, tile), tile)
-            gate = dot(x_v[at, :], wg_v[slot])
-            up = dot(x_v[at, :], wu_v[slot])
-            act_v[...] = (jax.nn.gelu(gate, approximate=True) * up).astype(BF16)
+        for m in range(tiles):
+            at = pl.ds(m * tile, tile)
+            expand(x_v.at[at], wg_v.at[slot], wu_v.at[slot], act_v.at[m % 2])
             for n in range(0, width, unit):
-                acc_v[at, n : n + unit] += dot(act_v[...], wd_v[slot, :, n : n + unit])
-
-            @pl.when(s == steps - 1)
-            def _():
-                h_copy(m).start()
-
-                @pl.when(m > 0)
-                def _():
-                    finish(m - 1)
-
-    finish(tiles - 1)
+                acc_v[at, n : n + unit] += dot(act_v[m % 2], wd_v[slot, :, n : n + unit])
+
+    for m in range(tiles):
+
+        @pl.loop(0, tile // 96)
+        def _(i):
+            at = span(m * (tile // 96) + i, 96)
+            x_v[at, :] = acc_v[at, :].astype(BF16)
+
+        out_copy(m).start()
+
+    for j in (pieces - 2, pieces - 1):
+        wait_recv(core_b(j))
     wait_send(own_copies())
 
     @pl.loop(0, pieces)
@@ -572,11 +610,11 @@
         out_copy(m).wait()
 
 
-def mlp(h1, norm_mlp, w_gate, w_up, w_down):
-    rows, width = h1.shape
+def mlp(x2, w_gate, w_up, w_down):
+    rows, width = x2.shape
     ff = w_gate.shape[1]
     unit = 512
-    tile = rows // 3
+    tile = rows // 6
     far = ff // 2 // unit
     pieces = 2 * far
     shapes = [(rows, width), (width, ff), (width, ff), (ff, width), (4, far, width, unit), (4, far, width, unit), (4, far, unit, width)]
@@ -584,13 +622,13 @@
     dma = pltpu.SemaphoreType.DMA
     out = pl.pallas_call(
         mlp_kernel,
-        in_specs=[pl.BlockSpec(memory_space=pltpu.VMEM)] + [any_spec] * 4,
+        in_specs=[any_spec] * 4,
         out_specs=[any_spec] * 7,
         out_shape=[jax.ShapeDtypeStruct(s, BF16) for s in shapes],
         scratch_shapes=[
             pltpu.VMEM((rows, width), BF16),
             pltpu.VMEM((rows, width), F32),
-            pltpu.VMEM((tile, unit), BF16),
+            pltpu.VMEM((2, tile, unit), BF16),
             pltpu.VMEM((2, width, unit), BF16),
             pltpu.VMEM((2, width, unit), BF16),
             pltpu.VMEM((2, unit, width), BF16),
@@ -604,8 +642,62 @@
         compiler_params=pltpu.CompilerParams(vmem_limit_bytes=VMEM_LIMIT, collective_id=0, has_side_effects=True),
         cost_estimate=pl.CostEstimate(flops=2 * rows * width * ff * 3 * 4, bytes_accessed=4 * 3 * width * ff * 2, transcendentals=0),
         name="mlp",
-    )(norm_mlp.reshape(1, width), h1, w_gate, w_up, w_down)
-    return out[0]
+    )(x2, w_gate, w_up, w_down)
+    return out[0], out[4:]
+
+
+def last_kernel(x_ref, part_ref, h_ref, wg_ref, wu_ref, wd_ref, key_hbm, value_hbm, out_ref, key_out, value_out, act_v, cache_v, sem):
+    i = pl.program_id(0)
+    pairs = ((key_hbm, key_out), (value_hbm, value_out))
+    loads = [pltpu.make_async_copy(src, cache_v.at[n], sem.at[n]) for n, (src, _) in enumerate(pairs)]
+    stores = [pltpu.make_async_copy(cache_v.at[n], dst, sem.at[n]) for n, (_, dst) in enumerate(pairs)]
+
+    @pl.when(i == 0)
+    def _():
+        start(loads)
+
+    @pl.when(i == 1)
+    def _():
+        for load, store in zip(loads, stores):
+            load.wait()
+            store.start()
+
+    expand(x_ref, wg_ref.at[0, 0], wu_ref.at[0, 0], act_v)
+    block = 512
+    for n in range(0, out_ref.shape[1], block):
+        at = slice(n, n + block)
+        total = part_ref[:, at].astype(F32) + dot(act_v[...], wd_ref[0, 0, :, at])
+        out_ref[:, at] = (h_ref[:, at].astype(F32) + total.astype(BF16).astype(F32)).astype(BF16)
+
+    @pl.when(i == pl.num_programs(0) - 1)
+    def _():
+        for store in stores:
+            store.wait()
+
+
+def finish(x2, part, h1, far_weights, key, value):
+    rows, width = x2.shape
+    tile = rows // 6
+    groups, per_group = far_weights[0].shape[:2]
+    row_block = pl.BlockSpec((tile, width), lambda i: (i, 0))
+    any_spec = pl.BlockSpec(memory_space=pl.ANY)
+
+    def weight_block(w):
+        return pl.BlockSpec((1, 1) + w.shape[2:], lambda i: (groups - 1, per_group - 1, 0, 0), pipeline_mode=pl.Buffered(1))
+
+    unit = far_weights[0].shape[3]
+    shape = jax.ShapeDtypeStruct
+    return pl.pallas_call(
+        last_kernel,
+        grid=(rows // tile,),
+        in_specs=[row_block] * 3 + [weight_block(w) for w in far_weights] + [any_spec] * 2,
+        out_specs=[row_block, any_spec, any_spec],
+        out_shape=[shape(x2.shape, BF16), shape(key.shape, BF16), shape(value.shape, BF16)],
+        scratch_shapes=[pltpu.VMEM((tile, unit), BF16), pltpu.VMEM((2,) + key.shape, BF16), pltpu.SemaphoreType.DMA((2,))],
+        compiler_params=pltpu.CompilerParams(dimension_semantics=("arbitrary",), vmem_limit_bytes=60 << 20),
+        cost_estimate=pl.CostEstimate(flops=6 * rows * width * unit, bytes_accessed=8 * rows * width, transcendentals=0),
+        name="finish",
+    )(x2, part, h1, *far_weights, key, value)
 
 
 def solution(mesh):
@@ -614,8 +706,11 @@
     arg_specs = (row_spec, P("dp"), P("dp"), P(), P(None, "tp"), P(), P(), P("tp", None), P(), P(None, "tp"), P(None, "tp"), P("tp", None))
 
     def local_layer(hidden, prefix_len, valid_len, norm_attn, w_query, w_key, w_value, w_out, norm_mlp, w_gate, w_up, w_down):
-        h1, key, value = attention(hidden, prefix_len, valid_len, norm_attn, w_query, w_key, w_value, w_out, tp_size)
-        out = mlp(h1.reshape(-1, hidden.shape[-1]), norm_mlp, w_gate, w_up, w_down)
+        h1, x2, key, value = attention(hidden, prefix_len, valid_len, norm_attn, norm_mlp, w_query, w_key, w_value, w_out, tp_size)
+        flat = (-1, hidden.shape[-1])
+        x2 = x2.reshape(flat)
+        part, far_weights = mlp(x2, w_gate, w_up, w_down)
+        out, key, value = finish(x2, part, h1.reshape(flat), far_weights, key, value)
         return out.reshape(hidden.shape), key, value
 
     return jax.shard_map(local_layer, mesh=mesh, in_specs=arg_specs, out_specs=(row_spec, row_spec, row_spec), check_vma=False)

time: 916 us -> 900 us (0.983)
  local copies, waits for them, and re-layouts: 16.8 us -> 0 us
    unnamed x7 -> x0, local copies, waits for them, and re-layouts: 14.3 us -> none
    pallas_call x2 -> x3, Pallas kernels: 898 us -> 899 us  [the longest x1 713 us: mlp(): pl.pallas_call(mlp_kernel, in_specs=[any_spec] * 4, out_specs=[any_spec]...]
where the time goes in v2:
time: 900 us
  Pallas kernels  899 us (100%)
    pallas_call x1, Pallas kernels, mlp(): pl.pallas_call(mlp_kernel, in_specs=[any_spec] * 4, out_specs=[any_spec]...  713 us
    pallas_call x1, Pallas kernels, attention(): pl.pallas_call(attention_kernel, in_specs=[smem, smem, vmem, vmem, any_sp...  153 us
    pallas_call x1, Pallas kernels, finish(): pl.pallas_call(last_kernel, grid=(rows // tile,), in_specs=[row_block] *...  33.2 us

profile of v2, /device:TPU:1, one launch (start us, length us, event | category | flops | bytes accessed | tf_op | source)
XLA Modules:
  0.0 899.6 jit_solution(8837924907729721854)
XLA Ops:
  0.6 152.6 %attention.1 = (bf16[12,288,2048]{2,1,0:T(8,128)(2,1)}, bf16[12,288,2048]{2,1,0:T(8,128)(2,1)}, bf16[12,288,256]{2,1,0:T(8,128)(2,1)}, bf16[12,288,256]{2,1,0:T(8,128)(2,1)}, bf16[1536,2048]{1,0:T(8,128)(2,1)}) custom-call(s32[12]{0:T(128)} %plen_ref.1, s32[12]{0:T(128)} %vlen_ref.1, bf16[2048]{0:T(1024)(128)(2,1)} %gain_ref.1, bf16[2048]{0:T(1024)(128)(2,1)} %gain2_ref.1, ...), custom_call_target="tpu_custom_call" | custom-call | flops 97844723712 | bytes 42467328 | tf_op jit(solution)/shard_map/attention/pallas_call | solution.py:397
  153.2 712.9 %mlp.1 = (bf16[3456,2048]{1,0:T(8,128)(2,1)}, bf16[2048,4096]{1,0:T(8,128)(2,1)}, bf16[2048,4096]{1,0:T(8,128)(2,1)}, bf16[4096,2048]{1,0:T(8,128)(2,1)}, bf16[4...) custom-call(bf16[3456,2048]{1,0:T(8,128)(2,1)} %bitcast.4, ...), custom_call_target="tpu_custom_call" | custom-call | flops 695784701952 | bytes 201326592 | tf_op jit(solution)/shard_map/mlp/pallas_call | solution.py:623
  866.1 33.2 %finish.1 = (bf16[3456,2048]{1,0:T(8,128)(2,1)}, bf16[12,288,256]{2,1,0:T(8,128)(2,1)}, bf16[12,288,256]{2,1,0:T(8,128)(2,1)}) custom-call(bf16[3456,2048]{1,0:T(8,128)(2,1)} %bitcast.5, bf16[3456,2048]{1,0:T(8,128)(2,1)} %get-tuple-element.15.part_ref, bf16[3456,2048]{1,0:T(8,128)(2,1)} %bitcast.3, bf16[4,4,2048,512]{3,2,1,0:T(8,128)(2,1)} %get-tuple-element.17.wg_ref, ...), custom_call_target="tpu_custom_call" | custom-call | flops 21743271936 | bytes 56623104 | tf_op jit(solution)/shard_map/finish/pallas_call | solution.py:690

commit v3 on v0

v3 whole, which is shorter than its diff:
```python
import functools

import jax
import jax.numpy as jnp
import numpy as np
from jax import lax
from jax.experimental import pallas as pl
from jax.experimental.pallas import tpu as pltpu
from jax.sharding import PartitionSpec as P

NORM_EPS = 1e-6
ROPE_BASE = 10000.0
MASK_FILL = -1e30
F32 = jnp.float32
BF16 = jnp.bfloat16
MESH = pl.DeviceIdType.MESH
VMEM_LIMIT = 67043328


def rope_tables(rows, blocks, head_dim):
    inv_freq = ROPE_BASE ** (-2.0 * np.arange(head_dim // 2) / head_dim)
    angles = np.arange(rows)[:, None] * inv_freq[None, :]
    starts = np.arange(blocks)[:, None] * rows * inv_freq[None, :]
    return tuple(f(a).astype(np.float32) for a in (angles, starts) for f in (np.cos, np.sin))


def normalize(rows, gain):
    inv = lax.rsqrt(jnp.mean(rows * rows, axis=-1, keepdims=True) + NORM_EPS)
    return (rows * inv * (1.0 + gain)).astype(BF16)


def dot(a, b):
    return jnp.dot(a, b, preferred_element_type=F32)


def span(index, size):
    return pl.ds(pl.multiple_of(index * size, size), size)


def start(copies):
    for c in copies:
        c.start()


def wait_recv(copies):
    for c in copies:
        c.wait_recv()


def wait_send(copies):
    for c in copies:
        c.wait_send()


def send(src, dst, send_sem, recv_sem, peer):
    return pltpu.make_async_remote_copy(src_ref=src, dst_ref=dst, send_sem=send_sem, recv_sem=recv_sem, device_id=peer, device_id_type=MESH)


def peers():
    dp = lax.axis_index("dp")
    tp = lax.axis_index("tp")
    core_tp = tp + 1 - 2 * lax.rem(tp, 2)
    chip_tp = lax.rem(tp + 2, 4)
    return dp, tp, chip_tp, {"tp": core_tp}, {"tp": chip_tp}, {"dp": 1 - dp}


def enter(*others):
    barrier = pltpu.get_barrier_semaphore()
    for peer in others:
        pl.semaphore_signal(barrier, inc=1, device_id=peer, device_id_type=MESH)
    pl.semaphore_wait(barrier, len(others))


Q_PIECES = 2
O_PIECES = 4


GELU_LINEAR = 0.7978845608028654
GELU_CUBIC = GELU_LINEAR * 0.044715


def expand(x_ref, gate_refs, up_refs, act_ref):
    for i, (gate_ref, up_ref) in enumerate(zip(gate_refs, up_refs)):
        block = gate_ref.shape[1]
        at = slice(i * block, (i + 1) * block)
        gate = dot(x_ref[...], gate_ref[...])
        up = dot(x_ref[...], up_ref[...])
        t = jnp.tanh(gate * (GELU_CUBIC * (gate * gate) + GELU_LINEAR))
        act_ref[:, at] = ((0.5 * gate) * up * (1.0 + t)).astype(BF16)


def layer_kernel(plen_ref, vlen_ref, gain_ref, gain2_ref, h_hbm, cos_ref, sin_ref, cos0_ref, sin0_ref, wq_hbm, wk_hbm, wv_hbm, wo_hbm, wg_hbm, wu_hbm, wd_hbm,
                 part_hbm, h1_hbm, x2_hbm, key_hbm, value_hbm, wo_far, pg_hbm, pu_hbm, pd_hbm, rg_hbm, ru_hbm, rd_hbm,
                 x_v, w_v, wd_v, act_v,
                 x_sem, wkv_sem, w_sem, out_sem, x2_sem, key_sem, load_sem, part_sem,
                 qc_send, qc_recv, qx_send, qx_recv, qy_send, qy_recv, qxc_send, qxc_recv, qyc_send, qyc_recv,
                 oc_send, oc_recv, ox_send, ox_recv, oy_send, oy_recv, oxc_send, oxc_recv, oyc_send, oyc_recv,
                 kx_send, kx_recv, kc_send, kc_recv, kxc_send, kxc_recv,
                 p_send, p_recv, a_send, a_recv, ac_send, ac_recv, b_send, b_recv, bc_send, bc_recv):
    num_batch, rows, width = h_hbm.shape
    total = num_batch * rows
    hd = wk_hbm.shape[1]
    half = hd // 2
    own_heads = wq_hbm.shape[1] // hd
    heads = w_v.shape[0]
    seq = rows * heads // own_heads
    tile = act_v.shape[1]
    tiles = total // tile
    unit = act_v.shape[2]
    piece = unit // 2
    own = wg_hbm.shape[1] // unit
    groups, pieces = rg_hbm.shape[:2]
    steps = 2 * own + groups * pieces // 2 - 1
    dp, tp, chip_tp, core_peer, chip_peer, group_peer = peers()
    own_rows = span(tp, rows)
    chip_rows = span(chip_tp, rows)

    def piece_refs(group, j):
        return rg_hbm.at[group, j], ru_hbm.at[group, j], rd_hbm.at[group, j]

    def own_copies():
        refs = ((wg_hbm, pg_hbm), (wu_hbm, pu_hbm), (wd_hbm, pd_hbm))
        return [send(src, dst, p_send.at[i], p_recv.at[i], core_peer) for i, (src, dst) in enumerate(refs)]

    def chip_copies(j):
        at = pl.ds(pl.multiple_of(dp * pieces * piece + j * piece, piece), piece)
        src = (wg_hbm.at[:, at], wu_hbm.at[:, at], wd_hbm.at[at, :])
        return [send(s, d, a_send.at[j, i], a_recv.at[j, i], chip_peer) for i, (s, d) in enumerate(zip(src, piece_refs(0, j)))]

    def relay(j, source, target, send_sems, recv_sems, peer):
        pairs = zip(piece_refs(source, j), piece_refs(target, j))
        return [send(s, d, send_sems.at[j, i], recv_sems.at[j, i], peer) for i, (s, d) in enumerate(pairs)]

    def core_a(j):
        return relay(j, 0, 1, ac_send, ac_recv, core_peer)

    def group_a(j):
        return relay(j, 0, 2, b_send, b_recv, group_peer)

    def core_b(j):
        return relay(j, 2, 3, bc_send, bc_recv, core_peer)

    def load(srcs, slot):
        dsts = [w_v.at[4 * slot + i] for i in range(4)] + [wd_v.at[slot, pl.ds(i * piece, piece)] for i in range(2)]
        return [pltpu.make_async_copy(src, dst, load_sem.at[slot, i]) for i, (src, dst) in enumerate(zip(srcs, dsts))]

    def near_load(refs, u, slot):
        ats = [pl.ds(pl.multiple_of(u * unit + i * piece, piece), piece) for i in range(2)]
        return load([refs[0].at[:, at] for at in ats] + [refs[1].at[:, at] for at in ats] + [refs[2].at[at] for at in ats], slot)

    def own_load(u, slot):
        return near_load((wg_hbm, wu_hbm, wd_hbm), u, slot)

    def peer_load(u, slot):
        return near_load((pg_hbm, pu_hbm, pd_hbm), u - own, slot)

    def far_load(u, slot):
        g = lax.rem(u - 2 * own, groups)
        p = (u - 2 * own) // groups
        return load([ref.at[g, 2 * p + i] for ref in (rg_hbm, ru_hbm, rd_hbm) for i in range(2)], slot)

    def h1_store(s):
        return pltpu.make_async_copy(x_v.at[span(s, rows)], h1_hbm.at[s], out_sem.at[s])

    def x2_store(s):
        return pltpu.make_async_copy(x_v.at[span(s, rows)], x2_hbm.at[s], x2_sem.at[s])

    def attend(q_v, kv_v, wkv_v, cos_v, sin_v):

        wkv = [pltpu.make_async_copy(w, wkv_v.at[i], wkv_sem.at[i]) for i, w in enumerate((wk_hbm, wv_hbm))]
        own_q = [pltpu.make_async_copy(wq_hbm.at[:, pl.ds(i * hd, hd)], w_v.at[i], w_sem.at[i, 0]) for i in range(own_heads)]

        def x_load(s):
            return pltpu.make_async_copy(h_hbm.at[s], x_v.at[span(s, rows)], x_sem.at[s])

        def own_o(n):
            return pltpu.make_async_copy(wo_hbm.at[:, pl.ds(n * hd, hd)], w_v.at[n, pl.ds(0, own_heads * hd)], w_sem.at[n, 0])

        def far_o(n):
            size = (heads - own_heads) * hd
            return pltpu.make_async_copy(wo_far.at[:, pl.ds(n * hd, hd)], w_v.at[n, pl.ds(own_heads * hd, size)], w_sem.at[n, 1])

        q_core = [send(wq_hbm.at[:, pl.ds(i * hd, hd)], w_v.at[own_heads + i], qc_send.at[i], qc_recv.at[i], core_peer) for i in range(own_heads)]
        q_rows = width // Q_PIECES

        def q_chip(i):
            return send(wq_hbm.at[pl.ds(i * q_rows, q_rows), span(dp, hd)], w_v.at[4, pl.ds(i * q_rows, q_rows)], qx_send.at[i], qx_recv.at[i], chip_peer)

        def q_move(src, dst, i, send_sem, recv_sem, peer):
            at = pl.ds(i * q_rows, q_rows)
            return send(w_v.at[src, at], w_v.at[dst, at], send_sem.at[i], recv_sem.at[i], peer)

        def q_group(i):
            return q_move(4, 6, i, qy_send, qy_recv, group_peer)

        def q_chip_core(i):
            return q_move(4, 5, i, qxc_send, qxc_recv, core_peer)

        def q_group_core(i):
            return q_move(6, 7, i, qyc_send, qyc_recv, core_peer)

        own_width = own_heads * hd
        o_rows = hd // O_PIECES
        o_core = [send(wo_hbm, wo_far.at[pl.ds(0, own_width)], oc_send.at[0], oc_recv.at[0], core_peer)]

        def far_rows(slot, i):
            return wo_far.at[pl.ds((slot - own_heads) * hd + i * o_rows, o_rows)]

        def o_chip(i):
            src = wo_hbm.at[pl.ds(pl.multiple_of(dp * hd + i * o_rows, o_rows), o_rows)]
            return send(src, far_rows(4, i), ox_send.at[i], ox_recv.at[i], chip_peer)

        def o_group(i):
            return send(far_rows(4, i), far_rows(6, i), oy_send.at[i], oy_recv.at[i], group_peer)

        def o_chip_core(i):
            return send(far_rows(4, i), far_rows(5, i), oxc_send.at[i], oxc_recv.at[i], core_peer)

        def o_group_core(i):
            return send(far_rows(6, i), far_rows(7, i), oyc_send.at[i], oyc_recv.at[i], core_peer)

        def kv_chip(s):
            return send(kv_v.at[s, own_rows], kv_v.at[s, own_rows], kx_send.at[s], kx_recv.at[s], chip_peer)

        def kv_core(s):
            return send(kv_v.at[s, own_rows], kv_v.at[s, own_rows], kc_send.at[s], kc_recv.at[s], core_peer)

        def kv_chip_core(s):
            return send(kv_v.at[s, chip_rows], kv_v.at[s, chip_rows], kxc_send.at[s], kxc_recv.at[s], core_peer)

        def kv_stores(s):
            outs = ((key_hbm, 0), (value_hbm, hd))
            return [pltpu.make_async_copy(kv_v.at[s, own_rows, pl.ds(at, hd)], ref.at[s], key_sem.at[s, i]) for i, (ref, at) in enumerate(outs)]

        def kv_send(s):
            kv_chip(s).start()
            kv_core(s).start()
            start(kv_stores(s))

        x_load(0).start()
        start(wkv + own_q)

        @pl.loop(1, num_batch)
        def _(s):
            x_load(s).start()

        enter(core_peer, chip_peer, group_peer)
        start([q_chip(i) for i in range(Q_PIECES)])
        start(q_core)
        start([o_chip(i) for i in range(O_PIECES)])
        start(o_core)

        gain = gain_ref[...].astype(F32)
        cos0, sin0 = cos0_ref[pl.ds(tp, 1), :], sin0_ref[pl.ds(tp, 1), :]
        cos_v[...] = cos_ref[...] * cos0 - sin_ref[...] * sin0
        sin_v[...] = sin_ref[...] * cos0 + cos_ref[...] * sin0
        for c in wkv + own_q:
            c.wait()

        def rope(x, cos, sin):
            a, c = x[:, :half], x[:, half:]
            return a * cos - c * sin, c * cos + a * sin

        def store_query(q, cos, sin, at, slot):
            lo, hi = rope(q, cos, sin)
            shape = q_v[at, slot, :, :half].shape
            q_v[at, slot, :, :half] = lo.astype(BF16).reshape(shape)
            q_v[at, slot, :, half:] = hi.astype(BF16).reshape(shape)

        @pl.loop(0, num_batch)
        def _(s):
            @pl.when(s == 5)
            def _():
                q_chip(0).wait_recv()
                start([q_group(0), q_chip_core(0)])

            @pl.when(s == num_batch - 1)
            def _():
                for i in range(1, Q_PIECES):
                    q_chip(i).wait_recv()
                    start([q_group(i), q_chip_core(i)])

            @pl.when(s > 0)
            def _():
                kv_send(s - 1)

            x_load(s).wait()
            at = span(s, rows)
            xn = normalize(x_v[at, :].astype(F32), gain)
            x_v[at, :] = xn
            cos, sin = cos_v[...], sin_v[...]
            lo, hi = rope(dot(xn, wkv_v[0]), cos, sin)
            kv_v[s, own_rows, :half] = lo.astype(BF16)
            kv_v[s, own_rows, half:hd] = hi.astype(BF16)
            kv_v[s, own_rows, hd:] = dot(xn, wkv_v[1]).astype(BF16)
            for i in range(own_heads):
                store_query(dot(xn, w_v[i]), cos * hd**-0.5, sin * hd**-0.5, s, i)

        kv_send(num_batch - 1)

        group = 3

        @pl.loop(own_heads, heads)
        def _(slot):
            @pl.when(slot == 2)
            def _():
                wait_recv(q_core)

            @pl.when(slot == 3)
            def _():
                o_chip(0).wait_recv()
                start([o_group(0), o_chip_core(0)])

            @pl.when(slot == 5)
            def _():
                wait_recv([q_chip_core(i) for i in range(Q_PIECES)])
                o_chip(1).wait_recv()
                start([o_group(1), o_chip_core(1)])

            @pl.when(slot == 6)
            def _():
                for i in range(Q_PIECES):
                    q_group(i).wait_recv()
                    q_group_core(i).start()
                o_chip(2).wait_recv()
                start([o_group(2), o_chip_core(2)])

            @pl.when(slot == 7)
            def _():
                wait_recv([q_group_core(i) for i in range(Q_PIECES)])
                o_chip(3).wait_recv()
                start([o_group(3), o_chip_core(3)])

            @pl.loop(0, num_batch // group)
            def _(i):
                at = span(i, group)
                cos = jnp.concatenate([cos_v[...] * hd**-0.5] * group, axis=0)
                sin = jnp.concatenate([sin_v[...] * hd**-0.5] * group, axis=0)
                store_query(dot(x_v[span(i, group * rows), :], w_v[slot]), cos, sin, at, slot)

        for copies in ([q_group(i) for i in range(Q_PIECES)], [q_chip_core(i) for i in range(Q_PIECES)], [q_group_core(i) for i in range(Q_PIECES)]):
            wait_send(copies)
        for n in range(heads):
            own_o(n).start()

        @pl.loop(0, num_batch)
        def _(s):
            x_load(s).start()

        kv_chip(0).wait_recv()
        kv_chip_core(0).start()
        for i in range(O_PIECES):
            o_group(i).wait_recv()
            o_group_core(i).start()
        wait_recv(o_core + [o_chip_core(i) for i in range(O_PIECES)] + [o_group_core(i) for i in range(O_PIECES)])
        for n in range(heads):
            far_o(n).start()

        tail = 128
        col = lax.broadcasted_iota(jnp.int32, (rows, tail), 1) + (seq - tail)
        row = lax.broadcasted_iota(jnp.int32, (rows, tail), 0) + tp * rows

        def score(s, p):
            return lax.dot_general(q_v[s, p], kv_v[s, :, :hd], (((1,), (1,)), ((), ())), preferred_element_type=F32)

        def probs(sc, allowed):
            sc = jnp.concatenate([sc[:, : seq - tail], jnp.where(allowed, sc[:, seq - tail :], MASK_FILL)], axis=1)
            p = jnp.exp(sc - jnp.max(sc, axis=-1, keepdims=True))
            return (p * (1.0 / jnp.sum(p, axis=-1, keepdims=True))).astype(BF16)

        def project(s, n):
            o = jnp.concatenate([q_v[s, j] for j in range(heads)], axis=1)
            at = span(s, rows), slice(n * hd, (n + 1) * hd)
            x_v[at] = (x_v[at].astype(F32) + dot(o, w_v[n]).astype(BF16).astype(F32)).astype(BF16)

        gain2 = gain2_ref[...].astype(F32)

        def norm_rows(s, first, size):
            at = pl.ds(pl.multiple_of(s * rows + first, 16), size)
            x_v[at, :] = normalize(x_v[at, :].astype(F32), gain2)

        @pl.loop(0, num_batch)
        def _(s):
            x_load(s).wait()

        for n in range(heads):
            own_o(n).wait()
            far_o(n).wait()

        last = num_batch - 1

        @pl.loop(0, num_batch)
        def _(s):
            before = lax.rem(s + last, num_batch)
            earlier = lax.rem(s + last - 2, num_batch)

            @pl.when(s < last)
            def _():
                kv_chip(s + 1).wait_recv()
                kv_chip_core(s + 1).start()

            @pl.when(s == last)
            def _():
                start(own_copies())

                @pl.loop(0, pieces)
                def _(j):
                    start(chip_copies(j))

            @pl.when(s == last - 2)
            def _():
                for i in range(last - 2, last + 1):
                    x_load(i).wait()

            @pl.when(s >= 3)
            def _():
                h1_store(s - 3).wait()

            wait_recv([kv_core(s), kv_chip_core(s)])
            allowed = (col < vlen_ref[s]) & ((col < plen_ref[s]) | (col <= row))
            sc = score(s, 0)
            for p in range(heads):
                ahead = score(s, p + 1) if p + 1 < heads else None
                project(before, p)
                if p < 6:
                    norm_rows(earlier, p * 48, 48)
                pr = probs(sc, allowed)
                q_v[s, p] = dot(pr, kv_v[s, :, hd:]).astype(BF16)
                sc = ahead

            @pl.when(s >= 1)
            def _():
                h1_store(s - 1).start()

            @pl.when(s >= 3)
            def _():
                x2_store(s - 3).start()

            @pl.when(s == 2)
            def _():
                for i in range(last - 2, last + 1):
                    x_load(i).start()

        for n in range(heads):
            project(last, n)
            if n == 3:
                start(own_load(0, 0))
        h1_store(last).start()
        for s in range(last - 2, last + 1):
            h1_store(s).wait()
            norm_rows(s, 0, rows)
            x2_store(s).start()

        wait_send(q_core + o_core + [q_chip(i) for i in range(Q_PIECES)])
        for i in range(O_PIECES):
            wait_send([o_chip(i), o_group(i), o_chip_core(i), o_group_core(i)])

        @pl.loop(0, num_batch)
        def _(s):
            wait_send([kv_chip(s), kv_core(s), kv_chip_core(s)])
            for c in kv_stores(s):
                c.wait()

    def feed_forward(acc_v):
        @pl.loop(0, total // 96)
        def _(i):
            acc_v[span(i, 96), :] = jnp.zeros((96, width), F32)

        def out_copy(m):
            at = span(m, tile)
            return pltpu.make_async_copy(x_v.at[at], part_hbm.at[at], part_sem.at[m])

        first_a, first_b, every = 3, 7, 3

        @pl.loop(0, steps)
        def _(s):
            slot = lax.rem(s, 2)

            @pl.when((s >= first_a) & (s < first_a + every * pieces) & (lax.rem(s, every) == first_a % every))
            def _():
                j = (s - first_a) // every
                wait_recv(chip_copies(j))
                start(group_a(j))
                start(core_a(j))

            @pl.when((s >= first_b) & (s < first_b + every * pieces) & (lax.rem(s, every) == first_b % every))
            def _():
                j = (s - first_b) // every
                wait_recv(group_a(j))
                start(core_b(j))

            u = s + 1

            @pl.when(u < own)
            def _():
                start(own_load(u, 1 - slot))

            @pl.when(u == own)
            def _():
                wait_recv(own_copies())

            @pl.when((u >= own) & (u < 2 * own))
            def _():
                start(peer_load(u, 1 - slot))

            @pl.when((u >= 2 * own) & (u < steps))
            def _():
                g = lax.rem(u - 2 * own, groups)
                p = (u - 2 * own) // groups

                @pl.when(g == 1)
                def _():
                    for j in (2 * p, 2 * p + 1):
                        wait_recv(core_a(j))

                @pl.when(g == 3)
                def _():
                    for j in (2 * p, 2 * p + 1):
                        wait_recv(core_b(j))

                start(far_load(u, 1 - slot))

            for c in own_load(0, slot):
                c.wait()

            gate = [w_v.at[4 * slot + i] for i in range(2)]
            up = [w_v.at[4 * slot + 2 + i] for i in range(2)]
            for m in range(tiles):
                at = pl.ds(m * tile, tile)
                expand(x_v.at[at], gate, up, act_v.at[m % 2])
                for n in range(0, width, unit):
                    acc_v[at, n : n + unit] += dot(act_v[m % 2], wd_v[slot, :, n : n + unit])

        @pl.loop(0, num_batch)
        def _(s):
            x2_store(s).wait()

        for m in range(tiles):

            @pl.loop(0, tile // 96)
            def _(i):
                at = span(m * (tile // 96) + i, 96)
                x_v[at, :] = acc_v[at, :].astype(BF16)

            out_copy(m).start()

        for j in (pieces - 2, pieces - 1):
            wait_recv(core_b(j))
        wait_send(own_copies())

        @pl.loop(0, pieces)
        def _(j):
            for copies in (chip_copies(j), group_a(j), core_a(j), core_b(j)):
                wait_send(copies)

        for m in range(tiles):
            out_copy(m).wait()

    pl.run_scoped(
        attend,
        pltpu.VMEM((num_batch, heads, rows, hd), BF16),
        pltpu.VMEM((num_batch, seq, 2 * hd), BF16),
        pltpu.VMEM((2, width, hd), BF16),
        pltpu.VMEM((rows, half), F32),
        pltpu.VMEM((rows, half), F32),
    )
    pl.run_scoped(feed_forward, pltpu.VMEM((total, width), F32))


def layer(hidden, prefix_len, valid_len, norm_attn, norm_mlp, w_query, w_key, w_value, w_out, w_gate, w_up, w_down, tp_size):
    num_batch, rows, width = hidden.shape
    total = num_batch * rows
    hd = w_key.shape[1]
    own_heads = w_query.shape[1] // hd
    heads = own_heads * tp_size
    seq = rows * tp_size
    ff = w_gate.shape[1]
    piece = 256
    pieces = ff // 2 // piece
    tile = total // 6
    tables = rope_tables(rows, tp_size, hd)
    any_spec = pl.BlockSpec(memory_space=pl.ANY)
    smem = pl.BlockSpec(memory_space=pltpu.SMEM)
    vmem = pl.BlockSpec(memory_space=pltpu.VMEM)
    dma = pltpu.SemaphoreType.DMA
    outs = [(total, width), (num_batch, rows, width), (num_batch, rows, width), (num_batch, rows, hd), (num_batch, rows, hd)]
    outs += [((heads - own_heads) * hd, width), (width, ff), (width, ff), (ff, width)]
    outs += [(4, pieces, width, piece), (4, pieces, width, piece), (4, pieces, piece, width)]
    flops = 2 * total * (width * (2 * heads + 2) * hd + 2 * heads * hd * seq + 3 * width * ff * tp_size)
    out = pl.pallas_call(
        layer_kernel,
        in_specs=[smem, smem, vmem, vmem, any_spec, vmem, vmem, vmem, vmem] + [any_spec] * 7,
        out_specs=[any_spec] * len(outs),
        out_shape=[jax.ShapeDtypeStruct(s, BF16) for s in outs],
        scratch_shapes=[
            pltpu.VMEM((total, width), BF16),
            pltpu.VMEM((heads, width, hd), BF16),
            pltpu.VMEM((2, 2 * piece, width), BF16),
            pltpu.VMEM((2, tile, 2 * piece), BF16),
            dma((num_batch,)),
            dma((2,)),
            dma((heads, 2)),
            dma((num_batch,)),
            dma((num_batch,)),
            dma((num_batch, 2)),
            dma((2, 6)),
            dma((total // tile,)),
        ]
        + [dma((own_heads,))] * 2
        + [dma((Q_PIECES,))] * 8
        + [dma((1,))] * 2
        + [dma((O_PIECES,))] * 8
        + [dma((num_batch,))] * 6
        + [dma((3,))] * 2
        + [dma((pieces, 3))] * 8,
        compiler_params=pltpu.CompilerParams(vmem_limit_bytes=VMEM_LIMIT, collective_id=0, has_side_effects=True),
        cost_estimate=pl.CostEstimate(flops=flops, bytes_accessed=8 * 3 * width * ff, transcendentals=total * (heads * seq + ff * tp_size)),
        name="layer",
    )(prefix_len, valid_len, norm_attn, norm_mlp, hidden, *(jnp.asarray(t) for t in tables), w_query, w_key, w_value, w_out, w_gate, w_up, w_down)
    return out[:5], out[9:]


def last_kernel(x_ref, part_ref, h_ref, wg_ref, wu_ref, wd_ref, key_hbm, value_hbm, out_ref, key_out, value_out, act_v, cache_v, sem):
    i = pl.program_id(0)
    pairs = ((key_hbm, key_out), (value_hbm, value_out))
    loads = [pltpu.make_async_copy(src, cache_v.at[n], sem.at[n]) for n, (src, _) in enumerate(pairs)]
    stores = [pltpu.make_async_copy(cache_v.at[n], dst, sem.at[n]) for n, (_, dst) in enumerate(pairs)]

    @pl.when(i == 0)
    def _():
        start(loads)

    @pl.when(i == 1)
    def _():
        for load, store in zip(loads, stores):
            load.wait()
            store.start()

    expand(x_ref, [wg_ref.at[0, n] for n in range(2)], [wu_ref.at[0, n] for n in range(2)], act_v)
    block = 512
    for n in range(0, out_ref.shape[1], block):
        at = slice(n, n + block)
        total = part_ref[:, at].astype(F32) + dot(act_v[...], wd_ref[0, :, :, at].reshape(act_v.shape[1], block))
        out_ref[:, at] = (h_ref[:, at].astype(F32) + total.astype(BF16).astype(F32)).astype(BF16)

    @pl.when(i == pl.num_programs(0) - 1)
    def _():
        for store in stores:
            store.wait()


def finish(x2, part, h1, far_weights, key, value):
    rows, width = x2.shape
    tile = rows // 6
    groups, pieces = far_weights[0].shape[:2]
    row_block = pl.BlockSpec((tile, width), lambda i: (i, 0))
    any_spec = pl.BlockSpec(memory_space=pl.ANY)

    def weight_block(w):
        return pl.BlockSpec((1, 2) + w.shape[2:], lambda i: (groups - 1, pieces // 2 - 1, 0, 0), pipeline_mode=pl.Buffered(1))

    unit = 2 * far_weights[0].shape[3]
    shape = jax.ShapeDtypeStruct
    return pl.pallas_call(
        last_kernel,
        grid=(rows // tile,),
        in_specs=[row_block] * 3 + [weight_block(w) for w in far_weights] + [any_spec] * 2,
        out_specs=[row_block, any_spec, any_spec],
        out_shape=[shape(x2.shape, BF16), shape(key.shape, BF16), shape(value.shape, BF16)],
        scratch_shapes=[pltpu.VMEM((tile, unit), BF16), pltpu.VMEM((2,) + key.shape, BF16), pltpu.SemaphoreType.DMA((2,))],
        compiler_params=pltpu.CompilerParams(dimension_semantics=("arbitrary",), vmem_limit_bytes=60 << 20),
        cost_estimate=pl.CostEstimate(flops=6 * rows * width * unit, bytes_accessed=8 * rows * width, transcendentals=0),
        name="finish",
    )(x2, part, h1, *far_weights, key, value)


def solution(mesh):
    tp_size = mesh.shape["tp"]
    row_spec = P("dp", "tp", None)
    arg_specs = (row_spec, P("dp"), P("dp"), P(), P(None, "tp"), P(), P(), P("tp", None), P(), P(None, "tp"), P(None, "tp"), P("tp", None))

    def local_layer(hidden, prefix_len, valid_len, norm_attn, w_query, w_key, w_value, w_out, norm_mlp, w_gate, w_up, w_down):
        (part, h1, x2, key, value), far_weights = layer(hidden, prefix_len, valid_len, norm_attn, norm_mlp, w_query, w_key, w_value, w_out, w_gate, w_up, w_down, tp_size)
        flat = (-1, hidden.shape[-1])
        out, key, value = finish(x2.reshape(flat), part, h1.reshape(flat), far_weights, key, value)
        return out.reshape(hidden.shape), key, value

    return jax.shard_map(local_layer, mesh=mesh, in_specs=arg_specs, out_specs=(row_spec, row_spec, row_spec), check_vma=False)
```

time: 2530 us -> 904 us (0.36)
  waiting for transfers between devices: 1350 us -> 0 us
  matrix products: 990 us -> 0 us
  Pallas kernels: 0 us -> 904 us
  other arithmetic: 107 us -> 0 us
  local copies, waits for them, and re-layouts: 50 us -> 0 us
    dot_general x7 -> x0, matrix products: 926 us -> none  [the longest x1 286 us: local_layer(): jnp.einsum('bsd,df->bsf', normed_mlp_full, w_gate, preferred_element_type...]
    pallas_call x0 -> x2, Pallas kernels: none -> 904 us  [the longest x1 870 us: layer(): pl.pallas_call(layer_kernel, in_specs=[smem, smem, vmem, vmem, any_spec,...]
    reduce_scatter x2 -> x0, waiting for transfers between devices: 726 us -> none  [the longest x1 363 us: local_layer(): mlp_out = lax.psum_scatter(mlp_part, 'tp', scatter_dimension=1, tiled=True)]
    all_gather x4 -> x0, waiting for transfers between devices: 629 us -> none  [the longest x1 331 us: local_layer(): normed_mlp_full = lax.all_gather(normed_mlp, 'tp', axis=1, tiled=True)]
    sub x1 -> x0, matrix products: 64.3 us -> none  [local_layer(): jax.nn.softmax(jnp.where(allowed[:, None], scores, MASK_FILL), axis=-1)]
    convert_element_type x4 -> x0, other arithmetic: 50.4 us -> none  [the longest x2 28.9 us: rms_norm(): (acts_f32 * inv_rms * (1.0 + norm_scale.astype(jnp.float32))).astype(jnp....]
    unnamed x14 -> x0, local copies, waits for them, and re-layouts: 31.2 us -> none
  transfers between devices with their start and end apart: 6 -> 0, of which waited for: 4 -> 0; matrix products, arithmetic and copies ran while one was open for 8% -> 0% of each run, Pallas kernels for 0% -> 0%
where the time goes in v3:
time: 904 us
  Pallas kernels  904 us (100%)
    pallas_call x1, Pallas kernels, layer(): pl.pallas_call(layer_kernel, in_specs=[smem, smem, vmem, vmem, any_spec,...  870 us
    pallas_call x1, Pallas kernels, finish(): pl.pallas_call(last_kernel, grid=(rows // tile,), in_specs=[row_block] *...  33.2 us

profile of v3, /device:TPU:1, one launch (start us, length us, event | category | flops | bytes accessed | tf_op | source)
XLA Modules:
  0.0 904.4 jit_solution(3977696488031414378)
XLA Ops:
  0.6 870.3 %layer.1 = (bf16[3456,2048]{1,0:T(8,128)(2,1)}, bf16[12,288,2048]{2,1,0:T(8,128)(2,1)}, bf16[12,288,2048]{2,1,0:T(8,128)(2,1)}, bf16[12,288,256]{2,1,0:T(8,128)(...) custom-call(s32[12]{0:T(128)} %plen_ref.1, ...), custom_call_target="tpu_custom_call" | custom-call | flops 793629425664 | bytes 201326592 | tf_op jit(solution)/shard_map/layer/pallas_call | solution.py:590
  870.9 33.2 %finish.1 = (bf16[3456,2048]{1,0:T(8,128)(2,1)}, bf16[12,288,256]{2,1,0:T(8,128)(2,1)}, bf16[12,288,256]{2,1,0:T(8,128)(2,1)}) custom-call(bf16[3456,2048]{1,0:T(8,128)(2,1)} %bitcast.4, bf16[3456,2048]{1,0:T(8,128)(2,1)} %get-tuple-element.15.part_ref, bf16[3456,2048]{1,0:T(8,128)(2,1)} %bitcast.3, bf16[4,8,2048,256]{3,2,1,0:T(8,128)(2,1)} %get-tuple-element.17.wg_ref, ...), custom_call_target="tpu_custom_call" | custom-call | flops 21743271936 | bytes 56623104 | tf_op jit(solution)/shard_map/finish/pallas_call | solution.py:664

commit v4 on v3

--- a/solution.py
+++ b/solution.py
@@ -370,7 +370,7 @@
 
         def project(s, n):
             o = jnp.concatenate([q_v[s, j] for j in range(heads)], axis=1)
-            at = span(s, rows), slice(n * hd, (n + 1) * hd)
+            at = span(s, rows), span(n, hd)
             x_v[at] = (x_v[at].astype(F32) + dot(o, w_v[n]).astype(BF16).astype(F32)).astype(BF16)
 
         gain2 = gain2_ref[...].astype(F32)
@@ -441,10 +441,15 @@
                 for i in range(last - 2, last + 1):
                     x_load(i).start()
 
-        for n in range(heads):
-            project(last, n)
-            if n == 3:
+        @pl.loop(0, heads // 2)
+        def _(i):
+            @pl.when(i == heads // 4)
+            def _():
                 start(own_load(0, 0))
+
+            project(last, 2 * i)
+            project(last, 2 * i + 1)
+
         h1_store(last).start()
         for s in range(last - 2, last + 1):
             h1_store(s).wait()
@@ -470,7 +475,7 @@
             at = span(m, tile)
             return pltpu.make_async_copy(x_v.at[at], part_hbm.at[at], part_sem.at[m])
 
-        first_a, first_b, every = 3, 7, 3
+        first_a, first_b, every = 4, 8, 3
 
         @pl.loop(0, steps)
         def _(s):
@@ -620,56 +625,105 @@
     return out[:5], out[9:]
 
 
-def last_kernel(x_ref, part_ref, h_ref, wg_ref, wu_ref, wd_ref, key_hbm, value_hbm, out_ref, key_out, value_out, act_v, cache_v, sem):
-    i = pl.program_id(0)
+def last_kernel(x_hbm, part_hbm, h_hbm, wg_hbm, wu_hbm, wd_hbm, key_hbm, value_hbm, out_hbm, key_out, value_out,
+                x_v, part_v, h_v, wg_v, wu_v, wd_v, act_v, cache_v, w_sem, row_sem, out_sem, cache_sem):
+    rows, width = x_v.shape
+    tile, unit = act_v.shape
+    tiles = rows // tile
+    groups, pieces = wg_hbm.shape[:2]
     pairs = ((key_hbm, key_out), (value_hbm, value_out))
-    loads = [pltpu.make_async_copy(src, cache_v.at[n], sem.at[n]) for n, (src, _) in enumerate(pairs)]
-    stores = [pltpu.make_async_copy(cache_v.at[n], dst, sem.at[n]) for n, (_, dst) in enumerate(pairs)]
-
-    @pl.when(i == 0)
-    def _():
-        start(loads)
-
-    @pl.when(i == 1)
-    def _():
-        for load, store in zip(loads, stores):
-            load.wait()
-            store.start()
-
-    expand(x_ref, [wg_ref.at[0, n] for n in range(2)], [wu_ref.at[0, n] for n in range(2)], act_v)
-    block = 512
-    for n in range(0, out_ref.shape[1], block):
-        at = slice(n, n + block)
-        total = part_ref[:, at].astype(F32) + dot(act_v[...], wd_ref[0, :, :, at].reshape(act_v.shape[1], block))
-        out_ref[:, at] = (h_ref[:, at].astype(F32) + total.astype(BF16).astype(F32)).astype(BF16)
-
-    @pl.when(i == pl.num_programs(0) - 1)
-    def _():
-        for store in stores:
-            store.wait()
+    loads = [pltpu.make_async_copy(src, cache_v.at[n], cache_sem.at[n]) for n, (src, _) in enumerate(pairs)]
+    stores = [pltpu.make_async_copy(cache_v.at[n], dst, cache_sem.at[n]) for n, (_, dst) in enumerate(pairs)]
+    weights = [
+        pltpu.make_async_copy(src.at[groups - 1, pl.ds(pieces - 2, 2)], dst, w_sem.at[n])
+        for n, (src, dst) in enumerate(((wg_hbm, wg_v), (wu_hbm, wu_v), (wd_hbm, wd_v)))
+    ]
+
+    def row_load(m, n):
+        at = span(m, tile)
+        src, dst = ((x_hbm, x_v), (part_hbm, part_v), (h_hbm, h_v))[n]
+        return pltpu.make_async_copy(src.at[at], dst.at[at], row_sem.at[m, n])
+
+    def out_store(m):
+        at = span(m, tile)
+        return pltpu.make_async_copy(h_v.at[at], out_hbm.at[at], out_sem.at[m])
+
+    row_load(0, 0).start()
+    start(weights[:2])
+    row_load(0, 0).wait()
+    for c in weights[:2]:
+        c.wait()
+    weights[2].start()
+    start([row_load(0, n) for n in (1, 2)])
+
+    @pl.loop(1, tiles)
+    def _(m):
+        start([row_load(m, n) for n in range(3)])
+
+    start(loads)
+
+    @pl.loop(0, tiles)
+    def _(m):
+        at = span(m, tile)
+
+        @pl.when(m == tiles // 2)
+        def _():
+            for load, store in zip(loads, stores):
+                load.wait()
+                store.start()
+
+        @pl.when(m > 0)
+        def _():
+            for n in range(3):
+                row_load(m, n).wait()
+
+        expand(x_v.at[at], [wg_v.at[n] for n in range(2)], [wu_v.at[n] for n in range(2)], act_v)
+
+        @pl.when(m == 0)
+        def _():
+            weights[2].wait()
+            for n in (1, 2):
+                row_load(0, n).wait()
+
+        block = 512
+        for n in range(0, width, block):
+            cols = slice(n, n + block)
+            total = part_v[at, cols].astype(F32) + dot(act_v[...], wd_v[:, :, cols].reshape(unit, block))
+            h_v[at, cols] = (h_v[at, cols].astype(F32) + total.astype(BF16).astype(F32)).astype(BF16)
+        out_store(m).start()
+
+    for store in stores:
+        store.wait()
+    for m in range(tiles):
+        out_store(m).wait()
 
 
 def finish(x2, part, h1, far_weights, key, value):
     rows, width = x2.shape
-    tile = rows // 6
-    groups, pieces = far_weights[0].shape[:2]
-    row_block = pl.BlockSpec((tile, width), lambda i: (i, 0))
+    tile = rows // 4
+    piece = far_weights[0].shape[3]
     any_spec = pl.BlockSpec(memory_space=pl.ANY)
-
-    def weight_block(w):
-        return pl.BlockSpec((1, 2) + w.shape[2:], lambda i: (groups - 1, pieces // 2 - 1, 0, 0), pipeline_mode=pl.Buffered(1))
-
-    unit = 2 * far_weights[0].shape[3]
+    dma = pltpu.SemaphoreType.DMA
     shape = jax.ShapeDtypeStruct
     return pl.pallas_call(
         last_kernel,
-        grid=(rows // tile,),
-        in_specs=[row_block] * 3 + [weight_block(w) for w in far_weights] + [any_spec] * 2,
-        out_specs=[row_block, any_spec, any_spec],
+        in_specs=[any_spec] * 8,
+        out_specs=[any_spec] * 3,
         out_shape=[shape(x2.shape, BF16), shape(key.shape, BF16), shape(value.shape, BF16)],
-        scratch_shapes=[pltpu.VMEM((tile, unit), BF16), pltpu.VMEM((2,) + key.shape, BF16), pltpu.SemaphoreType.DMA((2,))],
-        compiler_params=pltpu.CompilerParams(dimension_semantics=("arbitrary",), vmem_limit_bytes=60 << 20),
-        cost_estimate=pl.CostEstimate(flops=6 * rows * width * unit, bytes_accessed=8 * rows * width, transcendentals=0),
+        scratch_shapes=[pltpu.VMEM((rows, width), BF16)] * 3
+        + [
+            pltpu.VMEM((2, width, piece), BF16),
+            pltpu.VMEM((2, width, piece), BF16),
+            pltpu.VMEM((2, piece, width), BF16),
+            pltpu.VMEM((tile, 2 * piece), BF16),
+            pltpu.VMEM((2,) + key.shape, BF16),
+            dma((3,)),
+            dma((rows // tile, 3)),
+            dma((rows // tile,)),
+            dma((2,)),
+        ],
+        compiler_params=pltpu.CompilerParams(vmem_limit_bytes=VMEM_LIMIT),
+        cost_estimate=pl.CostEstimate(flops=12 * rows * width * piece, bytes_accessed=8 * rows * width, transcendentals=0),
         name="finish",
     )(x2, part, h1, *far_weights, key, value)
 

time: 904 us -> 906 us (level)
  no operation moved by 1% of the time
where the time goes in v4:
time: 906 us
  Pallas kernels  905 us (100%)
    pallas_call x1, Pallas kernels, layer(): pl.pallas_call(layer_kernel, in_specs=[smem, smem, vmem, vmem, any_spec,...  871 us
    pallas_call x1, Pallas kernels, finish(): pl.pallas_call(last_kernel, in_specs=[any_spec] * 8, out_specs=[any_spec]...  34.1 us

profile of v4, /device:TPU:1, one launch (start us, length us, event | category | flops | bytes accessed | tf_op | source)
XLA Modules:
  0.0 906.2 jit_solution(13305229197638341329)
XLA Ops:
  0.6 871.3 %layer.1 = (bf16[3456,2048]{1,0:T(8,128)(2,1)}, bf16[12,288,2048]{2,1,0:T(8,128)(2,1)}, bf16[12,288,2048]{2,1,0:T(8,128)(2,1)}, bf16[12,288,256]{2,1,0:T(8,128)(...) custom-call(s32[12]{0:T(128)} %plen_ref.1, ...), custom_call_target="tpu_custom_call" | custom-call | flops 793629425664 | bytes 201326592 | tf_op jit(solution)/shard_map/layer/pallas_call | solution.py:595
  871.9 34.1 %finish.1 = (bf16[3456,2048]{1,0:T(8,128)(2,1)}, bf16[12,288,256]{2,1,0:T(8,128)(2,1)}, bf16[12,288,256]{2,1,0:T(8,128)(2,1)}) custom-call(bf16[3456,2048]{1,0:T(8,128)(2,1)} %bitcast.4, bf16[3456,2048]{1,0:T(8,128)(2,1)} %get-tuple-element.15.part_hbm, bf16[3456,2048]{1,0:T(8,128)(2,1)} %bitcast.3, bf16[4,8,2048,256]{3,2,1,0:T(8,128)(2,1)} %get-tuple-element.17.wg_hbm, ...), custom_call_target="tpu_custom_call" | custom-call | flops 21743271936 | bytes 56623104 | tf_op jit(solution)/shard_map/finish/pallas_call | solution.py:708

commit v5 on v2

--- a/solution.py
+++ b/solution.py
@@ -17,10 +17,10 @@
 VMEM_LIMIT = 67043328
 
 
-def rope_tables(rows, blocks, head_dim):
+def rope_tables(seq, block, head_dim):
     inv_freq = ROPE_BASE ** (-2.0 * np.arange(head_dim // 2) / head_dim)
-    angles = np.arange(rows)[:, None] * inv_freq[None, :]
-    starts = np.arange(blocks)[:, None] * rows * inv_freq[None, :]
+    angles = np.arange(block)[:, None] * inv_freq[None, :]
+    starts = np.arange(0, seq, block)[:, None] * inv_freq[None, :]
     return tuple(f(a).astype(np.float32) for a in (angles, starts) for f in (np.cos, np.sin))
 
 
@@ -73,6 +73,7 @@
 
 Q_PIECES = 2
 O_PIECES = 4
+LAST_UNITS = 1
 
 
 def attention_kernel(plen_ref, vlen_ref, gain_ref, gain2_ref, h_hbm, cos_ref, sin_ref, cos0_ref, sin0_ref, wq_hbm, wk_hbm, wv_hbm, wo_hbm,
@@ -175,9 +176,16 @@
     start(o_core)
 
     gain = gain_ref[...].astype(F32)
-    cos0, sin0 = cos0_ref[pl.ds(tp, 1), :], sin0_ref[pl.ds(tp, 1), :]
-    cos_v[...] = cos_ref[...] * cos0 - sin_ref[...] * sin0
-    sin_v[...] = sin_ref[...] * cos0 + cos_ref[...] * sin0
+    block = cos_ref.shape[0]
+    blocks = rows // block
+
+    @pl.loop(0, blocks)
+    def _(i):
+        first = pl.ds(tp * blocks + i, 1)
+        cos0, sin0 = cos0_ref[first, :], sin0_ref[first, :]
+        cos_v[span(i, block), :] = cos_ref[...] * cos0 - sin_ref[...] * sin0
+        sin_v[span(i, block), :] = sin_ref[...] * cos0 + cos_ref[...] * sin0
+
     for c in wkv + own_q:
         c.wait()
 
@@ -357,8 +365,11 @@
             x_load(last).start()
 
     x_load(last).wait()
-    for n in range(heads):
-        project(last, n)
+    @pl.loop(0, heads // 2)
+    def _(i):
+        project(last, 2 * i)
+        project(last, 2 * i + 1)
+
     h1_store(last).start()
     for s in (last - 1, last):
         slot = s % 2
@@ -387,7 +398,7 @@
     own_heads = w_query.shape[1] // hd
     heads = own_heads * tp_size
     seq = rows * tp_size
-    tables = rope_tables(rows, tp_size, hd)
+    tables = rope_tables(seq, 16, hd)
     any_spec = pl.BlockSpec(memory_space=pl.ANY)
     smem = pl.BlockSpec(memory_space=pltpu.SMEM)
     vmem = pl.BlockSpec(memory_space=pltpu.VMEM)
@@ -458,7 +469,7 @@
     own = wg_hbm.shape[1] // unit
     pieces = own // 2 * 2
     groups, per_group = rg_hbm.shape[:2]
-    steps = 2 * own + groups * per_group - 1
+    steps = 2 * own + groups * per_group - LAST_UNITS
     dp, tp, chip_tp, core_peer, chip_peer, group_peer = peers()
 
     def piece_refs(group, j):
@@ -508,8 +519,7 @@
         p = i // groups
         return load((rg_hbm.at[g, p], ru_hbm.at[g, p], rd_hbm.at[g, p]), slot)
 
-    for m in range(tiles):
-        x_copy(m).start()
+    x_copy(0).start()
     start(own_load(0, 0))
     enter(core_peer, chip_peer, group_peer)
     start(own_copies())
@@ -521,9 +531,6 @@
     @pl.loop(0, rows // 96)
     def _(i):
         acc_v[span(i, 96), :] = jnp.zeros((96, width), F32)
-
-    for m in range(tiles):
-        x_copy(m).wait()
 
     def out_copy(m):
         at = span(m, tile)
@@ -582,20 +589,40 @@
         for c in own_load(0, slot):
             c.wait()
 
-        for m in range(tiles):
-            at = pl.ds(m * tile, tile)
-            expand(x_v.at[at], wg_v.at[slot], wu_v.at[slot], act_v.at[m % 2])
+        def compute(m, at, act):
+            expand(x_v.at[at], wg_v.at[slot], wu_v.at[slot], act)
             for n in range(0, width, unit):
-                acc_v[at, n : n + unit] += dot(act_v[m % 2], wd_v[slot, :, n : n + unit])
-
-    for m in range(tiles):
-
-        @pl.loop(0, tile // 96)
-        def _(i):
-            at = span(m * (tile // 96) + i, 96)
-            x_v[at, :] = acc_v[at, :].astype(BF16)
-
-        out_copy(m).start()
+                acc_v[at, n : n + unit] += dot(act[...], wd_v[slot, :, n : n + unit])
+
+        @pl.when((s == 0) | (s == steps - 1))
+        def _():
+            @pl.when(s == 0)
+            def _():
+                x_copy(0).wait()
+                for m in range(1, tiles):
+                    x_copy(m).start()
+
+            @pl.loop(0, tiles)
+            def _(m):
+                @pl.when((s == 0) & (m > 0))
+                def _():
+                    x_copy(m).wait()
+
+                compute(m, span(m, tile), act_v.at[0])
+
+                @pl.when(s == steps - 1)
+                def _():
+                    @pl.loop(0, tile // 96)
+                    def _(i):
+                        at = span(m * (tile // 96) + i, 96)
+                        x_v[at, :] = acc_v[at, :].astype(BF16)
+
+                    out_copy(m).start()
+
+        @pl.when((s > 0) & (s < steps - 1))
+        def _():
+            for m in range(tiles):
+                compute(m, pl.ds(m * tile, tile), act_v.at[m % 2])
 
     for j in (pieces - 2, pieces - 1):
         wait_recv(core_b(j))

time: 900 us -> 897 us (level)
  no operation moved by 1% of the time
where the time goes in v5:
time: 897 us
  Pallas kernels  896 us (100%)
    pallas_call x1, Pallas kernels, mlp(): pl.pallas_call(mlp_kernel, in_specs=[any_spec] * 4, out_specs=[any_spec]...  710 us
    pallas_call x1, Pallas kernels, attention(): pl.pallas_call(attention_kernel, in_specs=[smem, smem, vmem, vmem, any_sp...  153 us
    pallas_call x1, Pallas kernels, finish(): pl.pallas_call(last_kernel, grid=(rows // tile,), in_specs=[row_block] *...  33.3 us

profile of v5, /device:TPU:1, one launch (start us, length us, event | category | flops | bytes accessed | tf_op | source)
XLA Modules:
  0.0 897.3 jit_solution(17900147355247233653)
XLA Ops:
  0.6 153.1 %attention.1 = (bf16[12,288,2048]{2,1,0:T(8,128)(2,1)}, bf16[12,288,2048]{2,1,0:T(8,128)(2,1)}, bf16[12,288,256]{2,1,0:T(8,128)(2,1)}, bf16[12,288,256]{2,1,0:T(8,128)(2,1)}, bf16[1536,2048]{1,0:T(8,128)(2,1)}) custom-call(s32[12]{0:T(128)} %plen_ref.1, s32[12]{0:T(128)} %vlen_ref.1, bf16[2048]{0:T(1024)(128)(2,1)} %gain_ref.1, bf16[2048]{0:T(1024)(128)(2,1)} %gain2_ref.1, ...), custom_call_target="tpu_custom_call" | custom-call | flops 97844723712 | bytes 42467328 | tf_op jit(solution)/shard_map/attention/pallas_call | solution.py:408
  153.7 710.1 %mlp.1 = (bf16[3456,2048]{1,0:T(8,128)(2,1)}, bf16[2048,4096]{1,0:T(8,128)(2,1)}, bf16[2048,4096]{1,0:T(8,128)(2,1)}, bf16[4096,2048]{1,0:T(8,128)(2,1)}, bf16[4...) custom-call(bf16[3456,2048]{1,0:T(8,128)(2,1)} %bitcast.4, ...), custom_call_target="tpu_custom_call" | custom-call | flops 695784701952 | bytes 201326592 | tf_op jit(solution)/shard_map/mlp/pallas_call | solution.py:650
  863.8 33.3 %finish.1 = (bf16[3456,2048]{1,0:T(8,128)(2,1)}, bf16[12,288,256]{2,1,0:T(8,128)(2,1)}, bf16[12,288,256]{2,1,0:T(8,128)(2,1)}) custom-call(bf16[3456,2048]{1,0:T(8,128)(2,1)} %bitcast.5, bf16[3456,2048]{1,0:T(8,128)(2,1)} %get-tuple-element.15.part_ref, bf16[3456,2048]{1,0:T(8,128)(2,1)} %bitcast.3, bf16[4,4,2048,512]{3,2,1,0:T(8,128)(2,1)} %get-tuple-element.17.wg_ref, ...), custom_call_target="tpu_custom_call" | custom-call | flops 21743271936 | bytes 56623104 | tf_op jit(solution)/shard_map/finish/pallas_call | solution.py:717

commit v6 on v5

--- a/solution.py
+++ b/solution.py
@@ -536,24 +536,23 @@
         at = span(m, tile)
         return pltpu.make_async_copy(x_v.at[at], out_hbm.at[at], out_sem.at[m])
 
-    first_a, first_b, every = 4, 8, 3
-
     @pl.loop(0, steps)
     def _(s):
         slot = lax.rem(s, 2)
 
-        @pl.when((s >= first_a) & (s < first_a + every * pieces) & (lax.rem(s - first_a + every, every) == 0))
-        def _():
-            j = (s - first_a) // every
-            wait_recv(chip_copies(j))
-            start(group_a(j))
-            start(core_a(j))
-
-        @pl.when((s >= first_b) & (s < first_b + every * pieces) & (lax.rem(s - first_b + 2 * every, every) == 0))
-        def _():
-            j = (s - first_b) // every
-            wait_recv(group_a(j))
-            start(core_b(j))
+        turn = (s - 3) // 3
+        both = ((s >= 7) & (s <= 16) & (lax.rem(s, 3) == 1)) | ((s >= 20) & (s <= 26) & (lax.rem(s, 3) == 2))
+
+        @pl.when((s == 3) | both)
+        def _():
+            wait_recv(chip_copies(turn))
+            start(group_a(turn))
+            start(core_a(turn))
+
+        @pl.when(both | (s == 29))
+        def _():
+            wait_recv(group_a(turn - 1))
+            start(core_b(turn - 1))
 
         u = s + 1
 

time: 897 us -> 903 us (level)
  no operation moved by 1% of the time
where the time goes in v6:
time: 903 us; the launch traced here: 902 us
  Pallas kernels  901 us (100%)
    pallas_call x1, Pallas kernels, mlp(): pl.pallas_call(mlp_kernel, in_specs=[any_spec] * 4, out_specs=[any_spec]...  715 us
    pallas_call x1, Pallas kernels, attention(): pl.pallas_call(attention_kernel, in_specs=[smem, smem, vmem, vmem, any_sp...  153 us
    pallas_call x1, Pallas kernels, finish(): pl.pallas_call(last_kernel, grid=(rows // tile,), in_specs=[row_block] *...  33.3 us

profile of v6, /device:TPU:1, one launch (start us, length us, event | category | flops | bytes accessed | tf_op | source)
XLA Modules:
  0.0 901.7 jit_solution(5635442006869543924)
XLA Ops:
  0.6 153.1 %attention.1 = (bf16[12,288,2048]{2,1,0:T(8,128)(2,1)}, bf16[12,288,2048]{2,1,0:T(8,128)(2,1)}, bf16[12,288,256]{2,1,0:T(8,128)(2,1)}, bf16[12,288,256]{2,1,0:T(8,128)(2,1)}, bf16[1536,2048]{1,0:T(8,128)(2,1)}) custom-call(s32[12]{0:T(128)} %plen_ref.1, s32[12]{0:T(128)} %vlen_ref.1, bf16[2048]{0:T(1024)(128)(2,1)} %gain_ref.1, bf16[2048]{0:T(1024)(128)(2,1)} %gain2_ref.1, ...), custom_call_target="tpu_custom_call" | custom-call | flops 97844723712 | bytes 42467328 | tf_op jit(solution)/shard_map/attention/pallas_call | solution.py:408
  153.7 714.5 %mlp.1 = (bf16[3456,2048]{1,0:T(8,128)(2,1)}, bf16[2048,4096]{1,0:T(8,128)(2,1)}, bf16[2048,4096]{1,0:T(8,128)(2,1)}, bf16[4096,2048]{1,0:T(8,128)(2,1)}, bf16[4...) custom-call(bf16[3456,2048]{1,0:T(8,128)(2,1)} %bitcast.4, ...), custom_call_target="tpu_custom_call" | custom-call | flops 695784701952 | bytes 201326592 | tf_op jit(solution)/shard_map/mlp/pallas_call | solution.py:649
  868.2 33.3 %finish.1 = (bf16[3456,2048]{1,0:T(8,128)(2,1)}, bf16[12,288,256]{2,1,0:T(8,128)(2,1)}, bf16[12,288,256]{2,1,0:T(8,128)(2,1)}) custom-call(bf16[3456,2048]{1,0:T(8,128)(2,1)} %bitcast.5, bf16[3456,2048]{1,0:T(8,128)(2,1)} %get-tuple-element.15.part_ref, bf16[3456,2048]{1,0:T(8,128)(2,1)} %bitcast.3, bf16[4,4,2048,512]{3,2,1,0:T(8,128)(2,1)} %get-tuple-element.17.wg_ref, ...), custom_call_target="tpu_custom_call" | custom-call | flops 21743271936 | bytes 56623104 | tf_op jit(solution)/shard_map/finish/pallas_call | solution.py:716
